TPU v7x, 32 devices: a whole 2x2x4 slice. The times are simulated.
32 devices in a mesh: gx: 2 (over x), gy: 4 (over y, core), gz: 4 (over z).
Axes of the slice: x: 2, y: 2, z: 4, core: 2. Of those that a mesh axis runs over, the one named last changes fastest.
Arguments:
- dual_rhs: float32 [2, 4, 4, 3, 300, 128], P('gx', 'gy', 'gz'), may hold values from -6 to 6
- local_flex: bfloat16 [2, 4, 4, 1800, 1800], P('gx', 'gy', 'gz'), as said below
- corner_coupling: bfloat16 [2, 4, 4, 24, 1800], P('gx', 'gy', 'gz'), may hold values from -0.375 to 0.375
- face_stiffness: bfloat16 [2, 4, 4, 6, 300, 300], P('gx', 'gy', 'gz'), as said below
- coarse_inverse: bfloat16 [27, 27], replicated, as said below
- corner_ids: int32 [2, 4, 4, 8], P('gx', 'gy', 'gz'), may hold values from -1 to 8, as said below
Outputs:
- multipliers: float32 [2, 4, 4, 3, 300, 128], P('gx', 'gy', 'gz')
- residual: float32 [2, 4, 4, 3, 300, 128], P('gx', 'gy', 'gz')
Inputs may be any that keep to these rules, and one draw needn't show every extreme that they name: `local_flex`: each subdomain's matrix is symmetric positive definite. `face_stiffness`: each face block is symmetric positive definite. `coarse_inverse`: symmetric positive definite. `corner_ids`: entry k = 4 kx + 2 ky + kz of subdomain (i, j, l) is the number of the corner at lattice point (i + kx, j + ky, l + kz) when that point has all coordinates strictly between 0 and the subdomain counts, else -1; the 9 interior corners are numbered by a permutation, so subdomains sharing a corner name the same node.
All inputs are finite; a program needn't handle non-finite values.
Results may differ from a plain program's by a relative error of at most 0.04.
Values may be sent and summed in bfloat16 or wider, within the bound.
A program may use at most 64 MiB of HBM per device.

v0:
```python
import functools

import jax
import jax.numpy as jnp
from jax import lax
from jax.experimental import pallas as pl
from jax.experimental.pallas import tpu as pltpu
from jax.sharding import PartitionSpec as P

ITERS = 3
AXES = ("gx", "gy", "gz")
F32 = jnp.float32
BF16 = jnp.bfloat16
MESH = pl.DeviceIdType.MESH


def round_up(value, unit):
    return (value + unit - 1) // unit * unit


def kernel(
    sizes,
    dims,
    rhs_hbm,
    flex_hbm,
    coup_hbm,
    stiff_hbm,
    cinv_hbm,
    ids_ref,
    mult_ref,
    resid_ref,
    rhs_v,
    flex_v,
    coup_v,
    k_own,
    k_nb,
    cinv_v,
    r_send,
    r_recv,
    casm_wide,
    casm_v,
    c_own,
    c_nb,
    corr_v,
    res_v,
    z_v,
    zflat,
    signed_v,
    imgflat,
    img_send,
    img_recv,
    dir_v,
    s_v,
    lam_v,
    coarse_a,
    coarse_b,
    energy_a,
    energy_b,
    local_sem,
    setup_send,
    setup_recv,
    halo_send,
    halo_recv,
    a_send,
    a_recv,
    b_send,
    b_recv,
    ea_send,
    ea_recv,
    eb_send,
    eb_recv,
):
    nx, ny, nz = sizes
    faces, width, cols, ncoarse, corners = dims
    total = faces * width
    ncq = c_own.shape[1]
    wide = c_own.shape[2]
    here = [lax.axis_index(name) for name in AXES]
    plane = nx * ny
    me_plane = here[0] * ny + here[1]
    has = []
    for axis in range(3):
        has.append(here[axis] > 0)
        has.append(here[axis] < sizes[axis] - 1)
    masks = [jnp.where(flag, 1.0, 0.0).astype(F32) for flag in has]

    def neighbour(face):
        axis = face // 2
        step = 1 if face % 2 else -1
        spot = jnp.clip(here[axis] + step, 0, sizes[axis] - 1)
        return {AXES[axis]: spot}

    def plane_peer(offset):
        index = lax.rem(me_plane + offset, plane)
        return {"gx": index // ny, "gy": lax.rem(index, ny)}

    def z_peer(offset):
        return {"gz": lax.rem(here[2] + offset, nz)}

    barrier = pltpu.get_barrier_semaphore()
    for offset in range(1, plane):
        pl.semaphore_signal(barrier, inc=1, device_id=plane_peer(offset), device_id_type=MESH)
    for offset in range(1, nz):
        pl.semaphore_signal(barrier, inc=1, device_id=z_peer(offset), device_id_type=MESH)

    loads = []
    for index, (src, dst) in enumerate(
        ((rhs_hbm, rhs_v), (coup_hbm, coup_v), (cinv_hbm, cinv_v), (stiff_hbm, k_own), (flex_hbm, flex_v))
    ):
        copy = pltpu.make_async_copy(src, dst, local_sem.at[index])
        copy.start()
        loads.append(copy)

    loads[0].wait()
    for axis in range(3):
        owned = rhs_v[axis, :, 0, :] * masks[2 * axis + 1]
        res_v[2 * axis + 1] = owned
        r_send[axis] = owned.astype(BF16)
    pl.semaphore_wait(barrier, plane - 1 + nz - 1)

    def remote(src, dst, send_sem, recv_sem, target):
        return pltpu.make_async_remote_copy(
            src_ref=src, dst_ref=dst, send_sem=send_sem, recv_sem=recv_sem, device_id=target, device_id_type=MESH
        )

    def rhs_copy(axis):
        return remote(
            r_send.at[axis], r_recv.at[axis], setup_send.at[0, 2 * axis + 1], setup_recv.at[0, 2 * axis],
            neighbour(2 * axis + 1),
        )

    def k_copy(face):
        return remote(
            k_own.at[face], k_nb.at[face ^ 1], setup_send.at[1, face], setup_recv.at[1, face ^ 1], neighbour(face)
        )

    def c_copy(face):
        return remote(
            c_own.at[face], c_nb.at[face ^ 1], setup_send.at[2, face], setup_recv.at[2, face ^ 1], neighbour(face)
        )

    def halo_copy(it, face):
        return remote(
            img_send.at[it, face], img_recv.at[it, face ^ 1], halo_send.at[it, face], halo_recv.at[it, face ^ 1],
            neighbour(face),
        )

    def when_has(face, action):
        @pl.when(has[face])
        def _():
            action()

    for axis in (2, 0, 1):
        when_has(2 * axis + 1, lambda axis=axis: rhs_copy(axis).start())
    loads[3].wait()
    for face in (4, 0, 2, 5, 1, 3):
        when_has(face, lambda face=face: k_copy(face).start())

    for face in range(faces):

        @pl.when(jnp.logical_not(has[face]))
        def _(face=face):
            k_nb[face] = jnp.zeros(k_nb.shape[1:], BF16)
            c_nb[face] = jnp.zeros(c_nb.shape[1:], BF16)
            for it in range(ITERS):
                img_recv[it, face] = jnp.zeros((width, cols), BF16)

    for axis in range(3):

        @pl.when(jnp.logical_not(has[2 * axis]))
        def _(axis=axis):
            r_recv[axis] = jnp.zeros((width, cols), BF16)

    loads[1].wait()
    lane = lax.broadcasted_iota(jnp.int32, (1, 3 * corners), 1)
    target_row = jnp.full((1, 3 * corners), -1, jnp.int32)
    for k in range(corners):
        node = ids_ref[k]
        mine = (lane >= 3 * k) & (lane < 3 * k + 3) & (node >= 0)
        target_row = jnp.where(mine, 3 * node + lane - 3 * k, target_row)
    rows = lax.broadcasted_iota(jnp.int32, (ncq, 3 * corners), 0)
    assembly = jnp.where(rows == target_row, 1.0, 0.0).astype(BF16)
    assembled = jnp.dot(assembly, coup_v[...], preferred_element_type=F32)
    casm_v[...] = assembled.astype(BF16)
    casm_wide[...] = jnp.zeros(casm_wide.shape, F32)
    casm_wide[:, 0:total] = assembled
    span = casm_wide.shape[1]
    lanes = lax.broadcasted_iota(jnp.int32, (ncq, wide), 1)
    for face in range(faces):
        start = face * width
        low = start // 128 * 128
        high = min(round_up(start + width, 128), span)
        piece = casm_wide[:, low:high]
        if start > low:
            piece = pltpu.roll(piece, (high - low) - (start - low), 1)
        piece = piece[:, 0:wide]
        c_own[face] = jnp.where(lanes < width, piece, 0.0).astype(BF16)
        when_has(face, lambda face=face: c_copy(face).start())

    for axis in range(3):
        when_has(2 * axis, lambda axis=axis: rhs_copy(axis).wait_recv())
        res_v[2 * axis] = -r_recv[axis].astype(F32)
    loads[2].wait()

    scalar_row = lax.broadcasted_iota(jnp.int32, (8, cols), 0)
    rho_now = None
    step_size = None
    for it in range(ITERS):
        last = it + 1 == ITERS
        rho_acc = jnp.zeros((1, cols), F32)
        if it == 0:
            for face in range(faces):
                when_has(face, lambda face=face: remote(
                    k_own.at[face], k_nb.at[face], setup_send.at[1, face], setup_recv.at[1, face], neighbour(face)
                ).wait_recv())
            for face in range(faces):
                k_nb[face] = (k_own[face].astype(F32) + k_nb[face].astype(F32)).astype(BF16)
        for face in range(faces):
            res = res_v[face]
            half = (0.5 * res).astype(BF16)
            z = jnp.dot(k_nb[face], half, preferred_element_type=F32)
            z = z * (0.5 * masks[face])
            z_v[face] = z
            zflat[face * width : (face + 1) * width, :] = z
            if face % 2:
                rho_acc = rho_acc + jnp.sum(res * z, axis=0, keepdims=True)
        signed = zflat[...].astype(BF16)
        signed_v[...] = signed
        if it == 0:
            loads[4].wait()
        coarse_part = jnp.dot(casm_v[...], signed, preferred_element_type=F32)
        coarse_a[it, 0] = coarse_part.astype(BF16)

        def a_copy(offset, it=it):
            return remote(
                coarse_a.at[it, 0], coarse_a.at[it, offset], a_send.at[it, offset], a_recv.at[it, offset],
                plane_peer(offset),
            )

        def b_copy(offset, it=it):
            return remote(
                coarse_b.at[it, 0], coarse_b.at[it, offset], b_send.at[it, offset], b_recv.at[it, offset],
                z_peer(offset),
            )

        def ea_copy(offset, it=it):
            return remote(
                energy_a.at[it, 0], energy_a.at[it, offset], ea_send.at[it, offset], ea_recv.at[it, offset],
                plane_peer(offset),
            )

        def eb_copy(offset, it=it):
            return remote(
                energy_b.at[it, 0], energy_b.at[it, offset], eb_send.at[it, offset], eb_recv.at[it, offset],
                z_peer(offset),
            )

        for offset in range(1, plane):
            a_copy(offset).start()

        energy_acc = jnp.zeros((8, cols), F32)
        cuts = [0] + [round_up(2 * a * width, 16) for a in range(1, faces // 2)] + [total]
        order = [faces // 2 - 1] + list(range(faces // 2 - 1))
        for position, axis in enumerate(order):
            begin, end = cuts[axis], cuts[axis + 1]
            image = jnp.dot(flex_v[begin:end, :], signed_v[...], preferred_element_type=F32)
            imgflat[begin:end, :] = image
            weighted = image * signed_v[begin:end, :].astype(F32)
            energy_acc = energy_acc + jnp.sum(weighted.reshape(-1, 8, cols), axis=0)
            for face in (2 * axis, 2 * axis + 1):
                img_send[it, face] = imgflat[face * width : (face + 1) * width, :].astype(BF16)
            for face in (2 * axis, 2 * axis + 1):
                if not last or face % 2 == 0:
                    when_has(face, lambda face=face, it=it: halo_copy(it, face).start())
        energy_row = jnp.sum(energy_acc, axis=0, keepdims=True)
        energy_a[it, 0] = jnp.where(scalar_row == 0, energy_row, jnp.where(scalar_row == 1, rho_acc, 0.0))
        for offset in range(1, plane):
            ea_copy(offset).start()

        part = coarse_a[it, 0].astype(F32)
        for offset in range(1, plane):
            a_copy(offset).wait_recv()
            part = part + coarse_a[it, offset].astype(F32)
        coarse_b[it, 0] = part.astype(BF16)
        for offset in range(1, nz):
            b_copy(offset).start()
        energy = energy_a[it, 0]
        for offset in range(1, plane):
            ea_copy(offset).wait_recv()
            energy = energy + energy_a[it, offset]
        energy_b[it, 0] = energy
        for offset in range(1, nz):
            eb_copy(offset).start()

        if it == 0:
            for face in range(faces):
                when_has(face, lambda face=face: remote(
                    c_own.at[face], c_nb.at[face], setup_send.at[2, face], setup_recv.at[2, face], neighbour(face)
                ).wait_recv())
                own = c_own[face].astype(F32)
                other = c_nb[face].astype(F32)
                stack = jnp.concatenate([own, -other] * (corr_v.shape[2] // (2 * ncq)), axis=0)
                corr_v[face] = stack.T[0:width].astype(BF16)

        coarse = part
        for offset in range(1, nz):
            b_copy(offset).wait_recv()
            coarse = coarse + coarse_b[it, offset].astype(F32)
        sol = jnp.dot(cinv_v[...], coarse[0:ncoarse].astype(BF16), preferred_element_type=F32)
        sol = jnp.concatenate([sol, jnp.zeros((ncq - ncoarse, cols), F32)], axis=0) if ncq > ncoarse else sol
        sol_hi = sol.astype(BF16)
        sol_lo = (sol - sol_hi.astype(F32)).astype(BF16)
        if corr_v.shape[2] == 4 * ncq:
            sol_parts = [jnp.concatenate([sol_hi, sol_hi, sol_lo, sol_lo], axis=0)]
        else:
            sol_parts = [jnp.concatenate([piece, piece], axis=0) for piece in (sol_hi, sol_lo)]
        coarse_energy = jnp.sum(coarse * sol, axis=0, keepdims=True)

        energy = energy_b[it, 0]
        for offset in range(1, nz):
            eb_copy(offset).wait_recv()
            energy = energy + energy_b[it, offset]
        rho = energy[1:2]
        energy = energy[0:1] + coarse_energy

        if it == 0:
            step_size = rho / energy
            beta = None
        else:
            beta = rho / rho_now
            step_size = rho / (energy - beta * rho / step_size)
        rho_now = rho

        for face in range(faces):
            if last and face % 2 == 0:
                continue
            when_has(face, lambda face=face, it=it: remote(
                img_send.at[it, face], img_recv.at[it, face], halo_send.at[it, face], halo_recv.at[it, face],
                neighbour(face),
            ).wait_recv())
        for face in range(faces):
            if last and face % 2 == 0:
                continue
            image = img_send[it, face].astype(F32) - img_recv[it, face].astype(F32)
            for piece in sol_parts:
                image = image + jnp.dot(corr_v[face], piece, preferred_element_type=F32)
            image = image * masks[face]
            if it > 0:
                image = image + beta * s_v[face]
            new_res = res_v[face] - step_size * image
            if last:
                resid_ref[face // 2, :, 0, :] = new_res
            else:
                s_v[face] = image
                res_v[face] = new_res
            if face % 2:
                axis = face // 2
                direction = z_v[face]
                if it > 0:
                    direction = direction + beta * dir_v[axis]
                if not last:
                    dir_v[axis] = direction
                moved = step_size * direction
                if it > 0:
                    moved = moved + lam_v[axis]
                if last:
                    mult_ref[axis, :, 0, :] = moved
                else:
                    lam_v[axis] = moved

    for axis in range(3):
        when_has(2 * axis + 1, lambda axis=axis: rhs_copy(axis).wait_send())
    for face in range(faces):
        when_has(face, lambda face=face: k_copy(face).wait_send())
        when_has(face, lambda face=face: c_copy(face).wait_send())
        for it in range(ITERS):
            if it + 1 < ITERS or face % 2 == 0:
                when_has(face, lambda face=face, it=it: halo_copy(it, face).wait_send())
    for it in range(ITERS):
        for offset in range(1, plane):
            remote(coarse_a.at[it, 0], coarse_a.at[it, offset], a_send.at[it, offset], a_recv.at[it, offset],
                   plane_peer(offset)).wait_send()
            remote(energy_a.at[it, 0], energy_a.at[it, offset], ea_send.at[it, offset], ea_recv.at[it, offset],
                   plane_peer(offset)).wait_send()
        for offset in range(1, nz):
            remote(coarse_b.at[it, 0], coarse_b.at[it, offset], b_send.at[it, offset], b_recv.at[it, offset],
                   z_peer(offset)).wait_send()
            remote(energy_b.at[it, 0], energy_b.at[it, offset], eb_send.at[it, offset], eb_recv.at[it, offset],
                   z_peer(offset)).wait_send()


def body(sizes, dual_rhs, local_flex, corner_coupling, face_stiffness, coarse_inverse, corner_ids):
    rhs = dual_rhs.reshape(dual_rhs.shape[3:5] + (1,) + dual_rhs.shape[5:])
    flex = local_flex[0, 0, 0]
    coupling = corner_coupling[0, 0, 0]
    stiffness = face_stiffness[0, 0, 0]
    ids = corner_ids[0, 0, 0]
    faces, width, _ = stiffness.shape
    cols = rhs.shape[3]
    ncoarse = coarse_inverse.shape[0]
    corners = ids.shape[0]
    total = faces * width
    ncq = round_up(ncoarse, 32)
    wide = round_up(width, 128)
    span = round_up((faces - 1) * width // 128 * 128 + max(round_up(width + 127, 128), wide), 128)
    nx, ny, nz = sizes
    plane = nx * ny
    dma = pltpu.SemaphoreType.DMA
    any_space = pl.BlockSpec(memory_space=pl.ANY)
    vmem = pl.BlockSpec(memory_space=pltpu.VMEM)
    smem = pl.BlockSpec(memory_space=pltpu.SMEM)
    out = jax.ShapeDtypeStruct(rhs.shape, F32)
    mult, resid = pl.pallas_call(
        functools.partial(kernel, sizes, (faces, width, cols, ncoarse, corners)),
        out_shape=(out, out),
        in_specs=[any_space] * 5 + [smem],
        out_specs=(vmem, vmem),
        scratch_shapes=[
            pltpu.VMEM(rhs.shape, F32),
            pltpu.VMEM(flex.shape, BF16),
            pltpu.VMEM(coupling.shape, BF16),
            pltpu.VMEM(stiffness.shape, BF16),
            pltpu.VMEM(stiffness.shape, BF16),
            pltpu.VMEM(coarse_inverse.shape, BF16),
            pltpu.VMEM((3, width, cols), BF16),
            pltpu.VMEM((3, width, cols), BF16),
            pltpu.VMEM((ncq, span), F32),
            pltpu.VMEM((ncq, total), BF16),
            pltpu.VMEM((faces, ncq, wide), BF16),
            pltpu.VMEM((faces, ncq, wide), BF16),
            pltpu.VMEM((faces, width, (4 if ncq <= 64 else 2) * ncq), BF16),
            pltpu.VMEM((faces, width, cols), F32),
            pltpu.VMEM((faces, width, cols), F32),
            pltpu.VMEM((total, cols), F32),
            pltpu.VMEM((total, cols), BF16),
            pltpu.VMEM((total, cols), F32),
            pltpu.VMEM((ITERS, faces, width, cols), BF16),
            pltpu.VMEM((ITERS, faces, width, cols), BF16),
            pltpu.VMEM((3, width, cols), F32),
            pltpu.VMEM((faces, width, cols), F32),
            pltpu.VMEM((3, width, cols), F32),
            pltpu.VMEM((ITERS, plane, ncq, cols), BF16),
            pltpu.VMEM((ITERS, nz, ncq, cols), BF16),
            pltpu.VMEM((ITERS, plane, 8, cols), F32),
            pltpu.VMEM((ITERS, nz, 8, cols), F32),
            dma((5,)),
            dma((3, faces)),
            dma((3, faces)),
            dma((ITERS, faces)),
            dma((ITERS, faces)),
            dma((ITERS, plane)),
            dma((ITERS, plane)),
            dma((ITERS, nz)),
            dma((ITERS, nz)),
            dma((ITERS, plane)),
            dma((ITERS, plane)),
            dma((ITERS, nz)),
            dma((ITERS, nz)),
        ],
        compiler_params=pltpu.CompilerParams(
            collective_id=0, has_side_effects=True, vmem_limit_bytes=62 * 1024 * 1024
        ),
    )(rhs, flex, coupling, stiffness, coarse_inverse, ids)
    return (mult.reshape(dual_rhs.shape), resid.reshape(dual_rhs.shape))


def solution(mesh):
    sizes = tuple(mesh.shape[name] for name in AXES)
    placed = (
        P("gx", "gy", "gz", None, None, None),
        P("gx", "gy", "gz", None, None),
        P("gx", "gy", "gz", None, None),
        P("gx", "gy", "gz", None, None, None),
        P(),
        P("gx", "gy", "gz", None),
    )
    return jax.shard_map(
        functools.partial(body, sizes),
        mesh=mesh,
        in_specs=placed,
        out_specs=(P("gx", "gy", "gz", None, None, None), P("gx", "gy", "gz", None, None, None)),
        check_vma=False,
    )
```

profile of v0, /device:TPU:0, one launch (start us, length us, event | category | flops | bytes accessed | tf_op | source)
XLA Modules:
  0.0 59.9 jit_solution(9290540436507298638)
XLA Ops:
  0.6 55.6 %shard_map.77 = (f32[3,300,1,128]{3,2,1,0:T(1,128)}, f32[3,300,1,128]{3,2,1,0:T(1,128)}) custom-call(f32[3,300,1,128]{3,2,1,0:T(1,128)} %bitcast.15, bf16[1800,1800]{1,0:T(8,128)(2,1)} %bitcast.11, bf16[24,1800]{1,0:T(8,128)(2,1)} %bitcast.16, bf16[6,300,300]{2,1,0:T(8,128)(2,1)} %bitcast.12, bf16[27,27]{1,0:T(8,128)(2,1)} %cinv_hbm.1, s32[8]{0:T(128)} %bitcast.17), custom_call_target="tpu_custom_call" | custom-call | tf_op jit(solution)/shard_map/pallas_call | solution.py:413
  56.2 1.8 %copy.12 = f32[1,1,1,3,300,128]{5,2,4,3,1,0:T(1,128)} copy(f32[1,1,1,3,300,128]{5,2,4,3,1,0:T(1,128)} %bitcast.14) | data formatting | bytes 921600
  58.0 1.8 %copy.13 = f32[1,1,1,3,300,128]{5,2,4,3,1,0:T(1,128)} copy(f32[1,1,1,3,300,128]{5,2,4,3,1,0:T(1,128)} %bitcast.13) | data formatting | bytes 921600
where the time goes:
time: 60.1 us; the launch traced here: 59.9 us
  Pallas kernels  55.6 us (93%)
  local copies, waits for them, and re-layouts  3.64 us (6%)
  between operations  0.64 us (1%)
    pallas_call x1, Pallas kernels, body(): pl.pallas_call(functools.partial(kernel, sizes, (faces, width, cols, ncoa...  55.6 us
    unnamed x2, local copies, waits for them, and re-layouts  3.64 us

commit v1 on v0

--- a/solution.py
+++ b/solution.py
@@ -44,14 +44,13 @@
     corr_v,
     res_v,
     z_v,
+    v_v,
+    half_v,
     zflat,
     signed_v,
     imgflat,
     img_send,
     img_recv,
-    dir_v,
-    s_v,
-    lam_v,
     coarse_a,
     coarse_b,
     energy_a,
@@ -114,7 +113,7 @@
     loads[0].wait()
     for axis in range(3):
         owned = rhs_v[axis, :, 0, :] * masks[2 * axis + 1]
-        res_v[2 * axis + 1] = owned
+        res_v[axis] = owned
         r_send[axis] = owned.astype(BF16)
     pl.semaphore_wait(barrier, plane - 1 + nz - 1)
 
@@ -199,15 +198,47 @@
 
     for axis in range(3):
         when_has(2 * axis, lambda axis=axis: rhs_copy(axis).wait_recv())
-        res_v[2 * axis] = -r_recv[axis].astype(F32)
     loads[2].wait()
 
+    def total_of(value):
+        return jnp.sum(value, axis=0, keepdims=True)
+
+    def exchange(buffer, it, mine, count, peer, send_sem, recv_sem):
+        bank = it % 2
+
+        def copy(offset, slot):
+            return remote(
+                buffer.at[bank, slot], buffer.at[bank, slot], send_sem.at[it, offset], recv_sem.at[it, offset],
+                peer(offset),
+            )
+
+        def start(value):
+            buffer[bank, mine] = value
+            for offset in range(1, count):
+                copy(offset, mine).start()
+
+        def finish():
+            for offset in range(1, count):
+                copy(offset, lax.rem(mine + count - offset, count)).wait_recv()
+            value = buffer[bank, 0]
+            for slot in range(1, count):
+                value = value + buffer[bank, slot]
+            return value
+
+        def drain():
+            for offset in range(1, count):
+                copy(offset, mine).wait_send()
+
+        return start, finish, drain
+
+    coarse_row = lax.broadcasted_iota(jnp.int32, (ncq, cols), 0)
     scalar_row = lax.broadcasted_iota(jnp.int32, (8, cols), 0)
-    rho_now = None
-    step_size = None
+    scale = None
+    shrink = None
+    moments = []
+    drains = []
     for it in range(ITERS):
         last = it + 1 == ITERS
-        rho_acc = jnp.zeros((1, cols), F32)
         if it == 0:
             for face in range(faces):
                 when_has(face, lambda face=face: remote(
@@ -215,48 +246,50 @@
                 ).wait_recv())
             for face in range(faces):
                 k_nb[face] = (k_own[face].astype(F32) + k_nb[face].astype(F32)).astype(BF16)
+        rows_out = []
+        nu_acc = jnp.zeros((1, cols), F32)
+        mix_acc = jnp.zeros((1, cols), F32)
         for face in range(faces):
-            res = res_v[face]
-            half = (0.5 * res).astype(BF16)
+            axis = face // 2
+            if it > 0:
+                half = half_v[face]
+            elif face % 2:
+                half = (0.5 * res_v[axis]).astype(BF16)
+            else:
+                half = (-0.5 * r_recv[axis].astype(F32)).astype(BF16)
             z = jnp.dot(k_nb[face], half, preferred_element_type=F32)
-            z = z * (0.5 * masks[face])
-            z_v[face] = z
+            z = z * (0.5 * masks[face]) if it == 0 else z * (masks[face] * scale)
             zflat[face * width : (face + 1) * width, :] = z
             if face % 2:
-                rho_acc = rho_acc + jnp.sum(res * z, axis=0, keepdims=True)
+                z_v[it, axis] = z
+                if it == 0:
+                    res = res_v[axis]
+                    nu_acc = nu_acc + total_of(res * res)
+                    mix_acc = mix_acc + total_of(res * z)
+                if last:
+                    mix_acc = mix_acc + total_of(z * v_v[it - 1, axis])
+        if it == 0:
+            moments.append(mix_acc)
+            rows_out = [nu_acc, mix_acc]
+        elif it == 1:
+            rows_out = [moments[1]]
+        if last:
+            moments.append(mix_acc)
         signed = zflat[...].astype(BF16)
         signed_v[...] = signed
         if it == 0:
             loads[4].wait()
         coarse_part = jnp.dot(casm_v[...], signed, preferred_element_type=F32)
-        coarse_a[it, 0] = coarse_part.astype(BF16)
-
-        def a_copy(offset, it=it):
-            return remote(
-                coarse_a.at[it, 0], coarse_a.at[it, offset], a_send.at[it, offset], a_recv.at[it, offset],
-                plane_peer(offset),
-            )
-
-        def b_copy(offset, it=it):
-            return remote(
-                coarse_b.at[it, 0], coarse_b.at[it, offset], b_send.at[it, offset], b_recv.at[it, offset],
-                z_peer(offset),
-            )
-
-        def ea_copy(offset, it=it):
-            return remote(
-                energy_a.at[it, 0], energy_a.at[it, offset], ea_send.at[it, offset], ea_recv.at[it, offset],
-                plane_peer(offset),
-            )
-
-        def eb_copy(offset, it=it):
-            return remote(
-                energy_b.at[it, 0], energy_b.at[it, offset], eb_send.at[it, offset], eb_recv.at[it, offset],
-                z_peer(offset),
-            )
-
-        for offset in range(1, plane):
-            a_copy(offset).start()
+        for index, row in enumerate(rows_out):
+            coarse_part = jnp.where(coarse_row == ncoarse + index, row, coarse_part)
+        if it >= 2:
+            for drain in drains[:2]:
+                drain()
+            drains = drains[2:]
+        start_a, finish_a, drain_a = exchange(coarse_a, it, me_plane, plane, plane_peer, a_send, a_recv)
+        start_b, finish_b, drain_b = exchange(coarse_b, it, here[2], nz, z_peer, b_send, b_recv)
+        drains.extend((drain_a, drain_b))
+        start_a(coarse_part)
 
         energy_acc = jnp.zeros((8, cols), F32)
         cuts = [0] + [round_up(2 * a * width, 16) for a in range(1, faces // 2)] + [total]
@@ -265,32 +298,28 @@
             begin, end = cuts[axis], cuts[axis + 1]
             image = jnp.dot(flex_v[begin:end, :], signed_v[...], preferred_element_type=F32)
             imgflat[begin:end, :] = image
-            weighted = image * signed_v[begin:end, :].astype(F32)
-            energy_acc = energy_acc + jnp.sum(weighted.reshape(-1, 8, cols), axis=0)
+            if last:
+                weighted = image * signed_v[begin:end, :].astype(F32)
+                energy_acc = energy_acc + jnp.sum(weighted.reshape(-1, 8, cols), axis=0)
             for face in (2 * axis, 2 * axis + 1):
                 img_send[it, face] = imgflat[face * width : (face + 1) * width, :].astype(BF16)
             for face in (2 * axis, 2 * axis + 1):
                 if not last or face % 2 == 0:
                     when_has(face, lambda face=face, it=it: halo_copy(it, face).start())
-        energy_row = jnp.sum(energy_acc, axis=0, keepdims=True)
-        energy_a[it, 0] = jnp.where(scalar_row == 0, energy_row, jnp.where(scalar_row == 1, rho_acc, 0.0))
-        for offset in range(1, plane):
-            ea_copy(offset).start()
-
-        part = coarse_a[it, 0].astype(F32)
-        for offset in range(1, plane):
-            a_copy(offset).wait_recv()
-            part = part + coarse_a[it, offset].astype(F32)
-        coarse_b[it, 0] = part.astype(BF16)
-        for offset in range(1, nz):
-            b_copy(offset).start()
-        energy = energy_a[it, 0]
-        for offset in range(1, plane):
-            ea_copy(offset).wait_recv()
-            energy = energy + energy_a[it, offset]
-        energy_b[it, 0] = energy
-        for offset in range(1, nz):
-            eb_copy(offset).start()
+        if last:
+            moments.append(total_of(energy_acc))
+            block = jnp.zeros((8, cols), F32)
+            for index, row in enumerate(moments):
+                block = jnp.where(scalar_row == index, row, block)
+            start_ea, finish_ea, drain_ea = exchange(energy_a, 0, me_plane, plane, plane_peer, ea_send, ea_recv)
+            start_eb, finish_eb, drain_eb = exchange(energy_b, 0, here[2], nz, z_peer, eb_send, eb_recv)
+            drains.extend((drain_ea, drain_eb))
+            start_ea(block)
+
+        part = finish_a()
+        start_b(part)
+        if last:
+            start_eb(finish_ea())
 
         if it == 0:
             for face in range(faces):
@@ -302,11 +331,18 @@
                 stack = jnp.concatenate([own, -other] * (corr_v.shape[2] // (2 * ncq)), axis=0)
                 corr_v[face] = stack.T[0:width].astype(BF16)
 
-        coarse = part
-        for offset in range(1, nz):
-            b_copy(offset).wait_recv()
-            coarse = coarse + coarse_b[it, offset].astype(F32)
-        sol = jnp.dot(cinv_v[...], coarse[0:ncoarse].astype(BF16), preferred_element_type=F32)
+        coarse = finish_b()
+        if it == 0:
+            nu0 = coarse[ncoarse : ncoarse + 1]
+            rho0 = coarse[ncoarse + 1 : ncoarse + 2]
+            full = nu0 / rho0
+            scale = 0.5 * full
+        elif it == 1:
+            shrink = (rho0 / nu0) * (rho0 / coarse[ncoarse : ncoarse + 1])
+        coarse_hi = coarse[0:ncoarse].astype(BF16)
+        coarse_lo = (coarse[0:ncoarse] - coarse_hi.astype(F32)).astype(BF16)
+        sol = jnp.dot(cinv_v[...], coarse_hi, preferred_element_type=F32)
+        sol = sol + jnp.dot(cinv_v[...], coarse_lo, preferred_element_type=F32)
         sol = jnp.concatenate([sol, jnp.zeros((ncq - ncoarse, cols), F32)], axis=0) if ncq > ncoarse else sol
         sol_hi = sol.astype(BF16)
         sol_lo = (sol - sol_hi.astype(F32)).astype(BF16)
@@ -314,22 +350,8 @@
             sol_parts = [jnp.concatenate([sol_hi, sol_hi, sol_lo, sol_lo], axis=0)]
         else:
             sol_parts = [jnp.concatenate([piece, piece], axis=0) for piece in (sol_hi, sol_lo)]
-        coarse_energy = jnp.sum(coarse * sol, axis=0, keepdims=True)
-
-        energy = energy_b[it, 0]
-        for offset in range(1, nz):
-            eb_copy(offset).wait_recv()
-            energy = energy + energy_b[it, offset]
-        rho = energy[1:2]
-        energy = energy[0:1] + coarse_energy
-
-        if it == 0:
-            step_size = rho / energy
-            beta = None
-        else:
-            beta = rho / rho_now
-            step_size = rho / (energy - beta * rho / step_size)
-        rho_now = rho
+        if last:
+            coarse_energy = total_of(coarse * sol)
 
         for face in range(faces):
             if last and face % 2 == 0:
@@ -338,35 +360,45 @@
                 img_send.at[it, face], img_recv.at[it, face], halo_send.at[it, face], halo_recv.at[it, face],
                 neighbour(face),
             ).wait_recv())
+        dots = [jnp.zeros((1, cols), F32) for _ in range(it + 1)]
         for face in range(faces):
             if last and face % 2 == 0:
                 continue
+            axis = face // 2
             image = img_send[it, face].astype(F32) - img_recv[it, face].astype(F32)
             for piece in sol_parts:
                 image = image + jnp.dot(corr_v[face], piece, preferred_element_type=F32)
             image = image * masks[face]
-            if it > 0:
-                image = image + beta * s_v[face]
-            new_res = res_v[face] - step_size * image
-            if last:
-                resid_ref[face // 2, :, 0, :] = new_res
-            else:
-                s_v[face] = image
-                res_v[face] = new_res
+            if not last:
+                half_v[face] = ((0.5 * shrink if it else 0.5) * image).astype(BF16)
             if face % 2:
-                axis = face // 2
-                direction = z_v[face]
-                if it > 0:
-                    direction = direction + beta * dir_v[axis]
+                v_v[it, axis] = image
                 if not last:
-                    dir_v[axis] = direction
-                moved = step_size * direction
-                if it > 0:
-                    moved = moved + lam_v[axis]
-                if last:
-                    mult_ref[axis, :, 0, :] = moved
-                else:
-                    lam_v[axis] = moved
+                    for index in range(it + 1):
+                        dots[index] = dots[index] + total_of(z_v[index, axis] * image)
+        if not last:
+            moments.extend(dots)
+
+    sums = finish_eb()
+    rho, g00, g01, g11, g12, g22 = [sums[index : index + 1] for index in range(6)]
+    g22 = g22 + coarse_energy
+    g02 = shrink * g11
+    b1 = full * g00
+    b2 = full * shrink * g01
+    low1 = g01 / g00
+    low2 = g02 / g00
+    pivot1 = g11 - low1 * g01
+    cross = g12 - low1 * g02
+    low3 = cross / pivot1
+    pivot2 = g22 - low2 * g02 - low3 * cross
+    y1 = b1 - low1 * rho
+    y2 = b2 - low2 * rho - low3 * y1
+    c2 = y2 / pivot2
+    c1 = y1 / pivot1 - low3 * c2
+    c0 = rho / g00 - low1 * c1 - low2 * c2
+    for axis in range(3):
+        mult_ref[axis, :, 0, :] = c0 * z_v[0, axis] + c1 * z_v[1, axis] + c2 * z_v[2, axis]
+        resid_ref[axis, :, 0, :] = res_v[axis] - c0 * v_v[0, axis] - c1 * v_v[1, axis] - c2 * v_v[2, axis]
 
     for axis in range(3):
         when_has(2 * axis + 1, lambda axis=axis: rhs_copy(axis).wait_send())
@@ -376,17 +408,19 @@
         for it in range(ITERS):
             if it + 1 < ITERS or face % 2 == 0:
                 when_has(face, lambda face=face, it=it: halo_copy(it, face).wait_send())
-    for it in range(ITERS):
-        for offset in range(1, plane):
-            remote(coarse_a.at[it, 0], coarse_a.at[it, offset], a_send.at[it, offset], a_recv.at[it, offset],
-                   plane_peer(offset)).wait_send()
-            remote(energy_a.at[it, 0], energy_a.at[it, offset], ea_send.at[it, offset], ea_recv.at[it, offset],
-                   plane_peer(offset)).wait_send()
-        for offset in range(1, nz):
-            remote(coarse_b.at[it, 0], coarse_b.at[it, offset], b_send.at[it, offset], b_recv.at[it, offset],
-                   z_peer(offset)).wait_send()
-            remote(energy_b.at[it, 0], energy_b.at[it, offset], eb_send.at[it, offset], eb_recv.at[it, offset],
-                   z_peer(offset)).wait_send()
+    for drain in drains:
+        drain()
+
+
+def store(mult_ref, resid_ref, mult_hbm, resid_hbm, sem):
+    copies = (
+        pltpu.make_async_copy(mult_ref, mult_hbm, sem.at[0]),
+        pltpu.make_async_copy(resid_ref, resid_hbm, sem.at[1]),
+    )
+    for copy in copies:
+        copy.start()
+    for copy in copies:
+        copy.wait()
 
 
 def body(sizes, dual_rhs, local_flex, corner_coupling, face_stiffness, coarse_inverse, corner_ids):
@@ -400,7 +434,7 @@
     ncoarse = coarse_inverse.shape[0]
     corners = ids.shape[0]
     total = faces * width
-    ncq = round_up(ncoarse, 32)
+    ncq = round_up(ncoarse + 2, 32)
     wide = round_up(width, 128)
     span = round_up((faces - 1) * width // 128 * 128 + max(round_up(width + 127, 128), wide), 128)
     nx, ny, nz = sizes
@@ -409,6 +443,11 @@
     any_space = pl.BlockSpec(memory_space=pl.ANY)
     vmem = pl.BlockSpec(memory_space=pltpu.VMEM)
     smem = pl.BlockSpec(memory_space=pltpu.SMEM)
+    hbm = pl.BlockSpec(memory_space=pltpu.HBM)
+
+    def in_hbm(operand):
+        return pltpu.with_memory_space_constraint(operand, pltpu.HBM)
+
     out = jax.ShapeDtypeStruct(rhs.shape, F32)
     mult, resid = pl.pallas_call(
         functools.partial(kernel, sizes, (faces, width, cols, ncoarse, corners)),
@@ -429,20 +468,19 @@
             pltpu.VMEM((faces, ncq, wide), BF16),
             pltpu.VMEM((faces, ncq, wide), BF16),
             pltpu.VMEM((faces, width, (4 if ncq <= 64 else 2) * ncq), BF16),
-            pltpu.VMEM((faces, width, cols), F32),
-            pltpu.VMEM((faces, width, cols), F32),
+            pltpu.VMEM((3, width, cols), F32),
+            pltpu.VMEM((ITERS, 3, width, cols), F32),
+            pltpu.VMEM((ITERS, 3, width, cols), F32),
+            pltpu.VMEM((faces, width, cols), BF16),
             pltpu.VMEM((total, cols), F32),
             pltpu.VMEM((total, cols), BF16),
             pltpu.VMEM((total, cols), F32),
             pltpu.VMEM((ITERS, faces, width, cols), BF16),
             pltpu.VMEM((ITERS, faces, width, cols), BF16),
-            pltpu.VMEM((3, width, cols), F32),
-            pltpu.VMEM((faces, width, cols), F32),
-            pltpu.VMEM((3, width, cols), F32),
-            pltpu.VMEM((ITERS, plane, ncq, cols), BF16),
-            pltpu.VMEM((ITERS, nz, ncq, cols), BF16),
-            pltpu.VMEM((ITERS, plane, 8, cols), F32),
-            pltpu.VMEM((ITERS, nz, 8, cols), F32),
+            pltpu.VMEM((2, plane, ncq, cols), F32),
+            pltpu.VMEM((2, nz, ncq, cols), F32),
+            pltpu.VMEM((1, plane, 8, cols), F32),
+            pltpu.VMEM((1, nz, 8, cols), F32),
             dma((5,)),
             dma((3, faces)),
             dma((3, faces)),
@@ -452,15 +490,23 @@
             dma((ITERS, plane)),
             dma((ITERS, nz)),
             dma((ITERS, nz)),
-            dma((ITERS, plane)),
-            dma((ITERS, plane)),
-            dma((ITERS, nz)),
-            dma((ITERS, nz)),
+            dma((1, plane)),
+            dma((1, plane)),
+            dma((1, nz)),
+            dma((1, nz)),
         ],
         compiler_params=pltpu.CompilerParams(
-            collective_id=0, has_side_effects=True, vmem_limit_bytes=62 * 1024 * 1024
+            collective_id=0, has_side_effects=True, vmem_limit_bytes=(28 if ncq <= 64 else 54) * 1024 * 1024
         ),
-    )(rhs, flex, coupling, stiffness, coarse_inverse, ids)
+    )(*[in_hbm(operand) for operand in (rhs, flex, coupling, stiffness, coarse_inverse, ids)])
+    mult, resid = pl.pallas_call(
+        store,
+        out_shape=(out, out),
+        in_specs=[vmem, vmem],
+        out_specs=(hbm, hbm),
+        scratch_shapes=[dma((2,))],
+        compiler_params=pltpu.CompilerParams(vmem_limit_bytes=1024 * 1024),
+    )(mult, resid)
     return (mult.reshape(dual_rhs.shape), resid.reshape(dual_rhs.shape))
 
 

time: 60.1 us -> 50.4 us (0.84)
  Pallas kernels: 55.6 us -> 49.6 us
  local copies, waits for them, and re-layouts: 3.64 us -> 0 us
    pallas_call x1, Pallas kernels: 55.6 us -> 48.6 us  [body(): pl.pallas_call(functools.partial(kernel, sizes, (faces, width, cols, ncoa...]
    unnamed x2 -> x0, local copies, waits for them, and re-layouts: 3.64 us -> none
    pallas_call x0 -> x1, Pallas kernels: none -> 0.94 us  [body(): pl.pallas_call(store, out_shape=(out, out), in_specs=[vmem, vmem], out_sp...]
where the time goes in v1:
time: 50.4 us; the launch traced here: 50.2 us
  Pallas kernels  49.6 us (98%)
  between operations  0.64 us (1%)
    pallas_call x1, Pallas kernels, body(): pl.pallas_call(functools.partial(kernel, sizes, (faces, width, cols, ncoa...  48.6 us

profile of v1, /device:TPU:0, one launch (start us, length us, event | category | flops | bytes accessed | tf_op | source)
XLA Modules:
  0.0 50.2 jit_solution(1995887659908970479)
XLA Ops:
  0.6 48.6 %shard_map.77 = (f32[3,300,1,128]{3,2,1,0:T(1,128)S(1)}, f32[3,300,1,128]{3,2,1,0:T(1,128)S(1)}) custom-call(f32[3,300,1,128]{3,2,1,0:T(1,128)} %bitcast.13, bf16[1800,1800]{1,0:T(8,128)(2,1)} %bitcast.11, bf16[24,1800]{1,0:T(8,128)(2,1)} %bitcast.14, bf16[6,300,300]{2,1,0:T(8,128)(2,1)} %bitcast.12, bf16[27,27]{1,0:T(8,128)(2,1)} %cinv_hbm.1, s32[8]{0:T(128)} %bitcast.15), custom_call_target="tpu_custom_call" | custom-call | tf_op jit(solution)/shard_map/pallas_call | solution.py:452
  49.3 0.9 %shard_map.78 = (f32[3,300,1,128]{3,2,1,0:T(1,128)}, f32[3,300,1,128]{3,2,1,0:T(1,128)}) custom-call(f32[3,300,1,128]{3,2,1,0:T(1,128)S(1)} %get-tuple-element.6.mult_ref, f32[3,300,1,128]{3,2,1,0:T(1,128)S(1)} %get-tuple-element.7.resid_ref), custom_call_target="tpu_custom_call" | custom-call | tf_op jit(solution)/shard_map/pallas_call | solution.py:502

commit v2 on v1

--- a/solution.py
+++ b/solution.py
@@ -19,6 +19,515 @@
 
 
 def kernel(
+    sizes,
+    dims,
+    rhs_hbm,
+    flex_hbm,
+    coup_hbm,
+    stiff_hbm,
+    cinv_hbm,
+    ids_ref,
+    mult_ref,
+    resid_ref,
+    rhs_v,
+    flex_v,
+    coup_v,
+    k_own,
+    k_nb,
+    cinv_v,
+    r_send,
+    r_recv,
+    k_sum,
+    k_pad,
+    p_send,
+    p_recv,
+    casm_wide,
+    casm_v,
+    c_own,
+    c_nb,
+    corr_v,
+    span_v,
+    lift_v,
+    hess_v,
+    res_v,
+    z_v,
+    v_v,
+    half_v,
+    mz_v,
+    zflat,
+    signed_v,
+    imgflat,
+    img_send,
+    img_recv,
+    coarse_a,
+    coarse_b,
+    energy_a,
+    energy_b,
+    local_sem,
+    setup_send,
+    setup_recv,
+    k_send,
+    k_recv,
+    halo_send,
+    halo_recv,
+    a_send,
+    a_recv,
+    b_send,
+    b_recv,
+    ea_send,
+    ea_recv,
+    eb_send,
+    eb_recv,
+):
+    nx, ny, nz = sizes
+    faces, width, cols, ncoarse, corners = dims
+    total = faces * width
+    ncq = c_own.shape[1]
+    wide = c_own.shape[2]
+    here = [lax.axis_index(name) for name in AXES]
+    plane = nx * ny
+    me_plane = here[0] * ny + here[1]
+    has = []
+    for axis in range(3):
+        has.append(here[axis] > 0)
+        has.append(here[axis] < sizes[axis] - 1)
+    masks = [jnp.where(flag, 1.0, 0.0).astype(F32) for flag in has]
+
+    def neighbour(face):
+        axis = face // 2
+        step = 1 if face % 2 else -1
+        spot = jnp.clip(here[axis] + step, 0, sizes[axis] - 1)
+        return {AXES[axis]: spot}
+
+    def plane_peer(offset):
+        index = lax.rem(me_plane + offset, plane)
+        return {"gx": index // ny, "gy": lax.rem(index, ny)}
+
+    def z_peer(offset):
+        return {"gz": lax.rem(here[2] + offset, nz)}
+
+    barrier = pltpu.get_barrier_semaphore()
+    for offset in range(1, plane):
+        pl.semaphore_signal(barrier, inc=1, device_id=plane_peer(offset), device_id_type=MESH)
+    for offset in range(1, nz):
+        pl.semaphore_signal(barrier, inc=1, device_id=z_peer(offset), device_id_type=MESH)
+
+    loads = []
+    for index, (src, dst) in enumerate(
+        ((rhs_hbm, rhs_v), (coup_hbm, coup_v), (cinv_hbm, cinv_v), (stiff_hbm, k_own), (flex_hbm, flex_v))
+    ):
+        copy = pltpu.make_async_copy(src, dst, local_sem.at[index])
+        copy.start()
+        loads.append(copy)
+
+    loads[0].wait()
+    for axis in range(3):
+        owned = rhs_v[axis, :, 0, :] * masks[2 * axis + 1]
+        res_v[axis] = owned
+        r_send[axis] = owned.astype(BF16)
+    pl.semaphore_wait(barrier, plane - 1 + nz - 1)
+
+    def remote(src, dst, send_sem, recv_sem, target):
+        return pltpu.make_async_remote_copy(
+            src_ref=src, dst_ref=dst, send_sem=send_sem, recv_sem=recv_sem, device_id=target, device_id_type=MESH
+        )
+
+    def rhs_copy(axis):
+        return remote(
+            r_send.at[axis], r_recv.at[axis], setup_send.at[0, 2 * axis + 1], setup_recv.at[0, 2 * axis],
+            neighbour(2 * axis + 1),
+        )
+
+    def product_copy(axis):
+        return remote(
+            p_send.at[axis], p_recv.at[axis], setup_send.at[1, 2 * axis + 1], setup_recv.at[1, 2 * axis],
+            neighbour(2 * axis + 1),
+        )
+
+    bands = [(low, min(low + 128, width)) for low in range(0, width, 128)]
+
+    def k_copy(face, index, landing=None):
+        low, high = bands[index]
+        window = (pl.ds(low, width - low), pl.ds(low, high - low))
+        landing = face ^ 1 if landing is None else landing
+        return remote(
+            k_own.at[(face, *window)], k_nb.at[(landing, *window)], k_send.at[face, index], k_recv.at[landing, index],
+            neighbour(face),
+        )
+
+    def k_start(face):
+        for index in range(len(bands)):
+            k_copy(face, index).start()
+
+    def k_wait(face):
+        for index in range(len(bands)):
+            k_copy(face, index, face).wait_recv()
+
+    def k_drain(face):
+        for index in range(len(bands)):
+            k_copy(face, index).wait_send()
+
+    def c_copy(face):
+        return remote(
+            c_own.at[face], c_nb.at[face ^ 1], setup_send.at[2, face], setup_recv.at[2, face ^ 1], neighbour(face)
+        )
+
+    def halo_copy(it, face):
+        return remote(
+            img_send.at[it, face], img_recv.at[it, face ^ 1], halo_send.at[it, face], halo_recv.at[it, face ^ 1],
+            neighbour(face),
+        )
+
+    def when_has(face, action):
+        @pl.when(has[face])
+        def _():
+            action()
+
+    for axis in (2, 0, 1):
+        when_has(2 * axis + 1, lambda axis=axis: rhs_copy(axis).start())
+    loads[3].wait()
+    for face in (4, 0, 2):
+        when_has(face, lambda face=face: k_start(face))
+    for axis in (2, 0, 1):
+        face = 2 * axis + 1
+        half = (0.5 * res_v[axis]).astype(BF16)
+        half_v[face] = half
+        product = jnp.dot(k_own[face], half, preferred_element_type=F32) * (0.5 * masks[face])
+        p_send[axis] = product.astype(BF16)
+        when_has(face, lambda axis=axis: product_copy(axis).start())
+
+    for face in range(faces):
+
+        @pl.when(jnp.logical_not(has[face]))
+        def _(face=face):
+            k_nb[face] = jnp.zeros(k_nb.shape[1:], BF16)
+            c_nb[face] = jnp.zeros(c_nb.shape[1:], BF16)
+            for it in range(ITERS):
+                img_recv[it, face] = jnp.zeros((width, cols), BF16)
+
+    for axis in range(3):
+
+        @pl.when(jnp.logical_not(has[2 * axis]))
+        def _(axis=axis):
+            r_recv[axis] = jnp.zeros((width, cols), BF16)
+            p_recv[axis] = jnp.zeros((width, cols), BF16)
+
+    loads[1].wait()
+    lane = lax.broadcasted_iota(jnp.int32, (1, 3 * corners), 1)
+    target_row = jnp.full((1, 3 * corners), -1, jnp.int32)
+    for k in range(corners):
+        node = ids_ref[k]
+        mine = (lane >= 3 * k) & (lane < 3 * k + 3) & (node >= 0)
+        target_row = jnp.where(mine, 3 * node + lane - 3 * k, target_row)
+    rows = lax.broadcasted_iota(jnp.int32, (ncq, 3 * corners), 0)
+    assembly = jnp.where(rows == target_row, 1.0, 0.0).astype(BF16)
+    assembled = jnp.dot(assembly, coup_v[...], preferred_element_type=F32)
+    casm_v[...] = assembled.astype(BF16)
+    casm_wide[...] = jnp.zeros(casm_wide.shape, F32)
+    casm_wide[:, 0:total] = assembled
+    span = casm_wide.shape[1]
+    lanes = lax.broadcasted_iota(jnp.int32, (ncq, wide), 1)
+    for face in range(faces):
+        start = face * width
+        low = start // 128 * 128
+        high = min(round_up(start + width, 128), span)
+        piece = casm_wide[:, low:high]
+        if start > low:
+            piece = pltpu.roll(piece, (high - low) - (start - low), 1)
+        piece = piece[:, 0:wide]
+        c_own[face] = jnp.where(lanes < width, piece, 0.0).astype(BF16)
+        when_has(face, lambda face=face: c_copy(face).start())
+    for face in (5, 1, 3):
+        when_has(face, lambda face=face: k_start(face))
+    k_pad[...] = jnp.zeros(k_pad.shape, F32)
+
+    loads[2].wait()
+
+    def total_of(value):
+        return jnp.sum(value, axis=0, keepdims=True)
+
+    def exchange(buffer, it, mine, count, peer, send_sem, recv_sem):
+        bank = it
+
+        def copy(offset, slot):
+            return remote(
+                buffer.at[bank, slot], buffer.at[bank, slot], send_sem.at[it, offset], recv_sem.at[it, offset],
+                peer(offset),
+            )
+
+        def start(value):
+            buffer[bank, mine] = value
+            for offset in range(1, count):
+                copy(offset, mine).start()
+
+        def finish():
+            for offset in range(1, count):
+                copy(offset, lax.rem(mine + count - offset, count)).wait_recv()
+            value = buffer[bank, 0]
+            for slot in range(1, count):
+                value = value + buffer[bank, slot]
+            return value
+
+        def drain():
+            for offset in range(1, count):
+                copy(offset, mine).wait_send()
+
+        return start, finish, drain
+
+    coarse_row = lax.broadcasted_iota(jnp.int32, (ncq, cols), 0)
+    scalar_row = lax.broadcasted_iota(jnp.int32, (8, cols), 0)
+    moments = []
+    drains = []
+    rounds = []
+
+    def reduction(value):
+        index = len(rounds)
+        start_a, finish_a, drain_a = exchange(coarse_a, index, me_plane, plane, plane_peer, a_send, a_recv)
+        start_b, finish_b, drain_b = exchange(coarse_b, index, here[2], nz, z_peer, b_send, b_recv)
+        drains.extend((drain_a, drain_b))
+        rounds.append(index)
+        start_a(value)
+        return lambda: start_b(finish_a()), finish_b
+
+    def with_rows(value, rows_out):
+        for index, row in enumerate(rows_out):
+            value = jnp.where(coarse_row == ncoarse + index, row, value)
+        return value
+
+    def split(value):
+        high = value.astype(BF16)
+        return high, (value - high.astype(F32)).astype(BF16)
+
+    def wait_halo(it, face):
+        when_has(face, lambda: remote(
+            img_send.at[it, face], img_recv.at[it, face], halo_send.at[it, face], halo_recv.at[it, face],
+            neighbour(face),
+        ).wait_recv())
+
+    def local_jump(it, face):
+        return img_send[it, face].astype(F32) - img_recv[it, face].astype(F32)
+
+    def full_image(it, axis, stack):
+        face = 2 * axis + 1
+        image = local_jump(it, face) + jnp.dot(corr_v[face], stack, preferred_element_type=F32)
+        image = image * masks[face]
+        v_v[it, axis] = image
+        return image
+
+    def solve_coarse(rhs):
+        high, low = split(rhs[0:ncoarse])
+        sol = jnp.dot(cinv_v[...], high, preferred_element_type=F32)
+        sol = sol + jnp.dot(cinv_v[...], low, preferred_element_type=F32)
+        if ncq > ncoarse:
+            sol = jnp.concatenate([sol, jnp.zeros((ncq - ncoarse, cols), F32)], axis=0)
+        high, low = split(sol)
+        return (
+            total_of(rhs * sol),
+            jnp.concatenate([high, high, low, low], axis=0),
+            jnp.concatenate([high, low, high, low], axis=0),
+        )
+
+    def prepare(face):
+        when_has(face, lambda: remote(
+            c_own.at[face], c_nb.at[face], setup_send.at[2, face], setup_recv.at[2, face], neighbour(face)
+        ).wait_recv())
+        both = jnp.concatenate([c_own[face], -c_nb[face]], axis=0)
+        wide_stack = jnp.concatenate([both, both], axis=0).astype(F32)
+        corr_v[face] = wide_stack.T[0:width].astype(BF16)
+        product = jnp.dot(both[:, 0:width], k_sum[face], preferred_element_type=F32)
+        spread = (product[0:ncq] + product[ncq : 2 * ncq]) * (0.25 * masks[face])
+        high, low = split(spread)
+        tall = jnp.concatenate([high, high, low, low], axis=0)
+        span_v[face, :, 0:width] = tall
+        lift_v[face] = span_v[face].astype(F32).T[0:width].astype(BF16)
+        if face % 2 == 0:
+            return None
+        product = lax.dot_general(
+            both[:, 0:width], tall, (((1,), (1,)), ((), ())), preferred_element_type=F32
+        )
+        product = product[0:ncq] + product[ncq : 2 * ncq]
+        return product + pltpu.roll(product, 2 * ncq, 1)
+
+    def flatten(face, z):
+        zflat[face * width : (face + 1) * width, :] = z
+
+    def add_stiffness(face):
+        when_has(face, lambda: k_wait(face))
+        for low, high in bands:
+            both = k_own[face, low:width, low:high].astype(F32) + k_nb[face, low:width, low:high].astype(F32)
+            k_sum[face, low:width, low:high] = both.astype(BF16)
+            if high < width:
+                k_pad[face % 2, low:width, 0 : high - low] = both
+                below = k_pad[face % 2, high : k_pad.shape[1], :].T
+                k_sum[face, low:high, high:width] = below[:, 0 : width - high].astype(BF16)
+
+    nu_acc = jnp.zeros((1, cols), F32)
+    rho_acc = jnp.zeros((1, cols), F32)
+    for axis in (2, 0, 1):
+        face = 2 * axis
+        when_has(face, lambda axis=axis: rhs_copy(axis).wait_recv())
+        half = (-0.5 * r_recv[axis].astype(F32)).astype(BF16)
+        mz_v[face] = jnp.dot(k_own[face], half, preferred_element_type=F32) * (0.5 * masks[face])
+    for axis in (2, 0, 1):
+        face = 2 * axis + 1
+        add_stiffness(face)
+        z = jnp.dot(k_sum[face], half_v[face], preferred_element_type=F32)
+        z = z * (0.5 * masks[face])
+        flatten(face, z)
+        z_v[0, axis] = z
+        res = res_v[axis]
+        nu_acc = nu_acc + total_of(res * res)
+        rho_acc = rho_acc + total_of(res * z)
+    for axis in (2, 0, 1):
+        face = 2 * axis
+        when_has(face, lambda axis=axis: product_copy(axis).wait_recv())
+        flatten(face, mz_v[face] - p_recv[axis].astype(F32))
+    moments.append(rho_acc)
+    signed = zflat[...].astype(BF16)
+    signed_v[...] = signed
+    part = jnp.dot(casm_v[...], signed, preferred_element_type=F32)
+    forward, finish = reduction(with_rows(part, [nu_acc, rho_acc]))
+    loads[4].wait()
+
+    cuts = [0] + [round_up(2 * a * width, 16) for a in range(1, faces // 2)] + [total]
+    order = [faces // 2 - 1] + list(range(faces // 2 - 1))
+    span_v[:, :, width:] = jnp.zeros((faces, 4 * ncq, wide - width), BF16)
+    scale = None
+    shrink = None
+    stack = None
+    for it in range(ITERS):
+        last = it + 1 == ITERS
+        energy_acc = jnp.zeros((8, cols), F32)
+        dots = [jnp.zeros((1, cols), F32) for _ in range(it + 1)]
+        for position, axis in enumerate(order):
+            begin, end = cuts[axis], cuts[axis + 1]
+            image = jnp.dot(flex_v[begin:end, :], signed_v[...], preferred_element_type=F32)
+            imgflat[begin:end, :] = image
+            if last:
+                weighted = image * signed_v[begin:end, :].astype(F32)
+                energy_acc = energy_acc + jnp.sum(weighted.reshape(-1, 8, cols), axis=0)
+            for face in (2 * axis, 2 * axis + 1):
+                img_send[it, face] = imgflat[face * width : (face + 1) * width, :].astype(BF16)
+            if it > 0:
+                whole = full_image(it - 1, axis, stack)
+                for index in range(it + 1):
+                    if index < it or last:
+                        dots[index] = dots[index] + total_of(z_v[index, axis] * whole)
+            for face in (2 * axis, 2 * axis + 1):
+                if not last or face % 2 == 0:
+                    when_has(face, lambda face=face, it=it: halo_copy(it, face).start())
+        if it > 0:
+            moments.extend(dots if last else dots[0:it])
+        if it == 0:
+            hess = jnp.zeros((ncq, cols), F32)
+            for axis in order:
+                hess = hess + prepare(2 * axis + 1)
+            forward()
+            for axis in order:
+                add_stiffness(2 * axis)
+                prepare(2 * axis)
+            forward_h, finish_h = reduction(hess)
+        else:
+            forward()
+        if last:
+            moments.append(total_of(energy_acc))
+            block = jnp.zeros((8, cols), F32)
+            for index, row in enumerate(moments):
+                block = jnp.where(scalar_row == index, row, block)
+            start_ea, finish_ea, drain_ea = exchange(energy_a, 0, me_plane, plane, plane_peer, ea_send, ea_recv)
+            start_eb, finish_eb, drain_eb = exchange(energy_b, 0, here[2], nz, z_peer, eb_send, eb_recv)
+            drains.extend((drain_ea, drain_eb))
+            start_ea(block)
+        else:
+            gather = jnp.zeros((2 * ncq, cols), F32)
+            own_energy = jnp.zeros((1, cols), F32)
+            for axis in order:
+                for face in (2 * axis, 2 * axis + 1):
+                    wait_halo(it, face)
+                    jump = local_jump(it, face)
+                    half = (0.5 * jump).astype(BF16)
+                    half_v[face] = half
+                    if face % 2:
+                        gather = gather + jnp.dot(
+                            span_v[face, ncq : 3 * ncq, 0:width], half, preferred_element_type=F32
+                        )
+                        if it == 0:
+                            own_energy = own_energy + total_of(z_v[0, axis] * jump * masks[face])
+            gather = 2.0 * (gather[0:ncq] + gather[ncq : 2 * ncq])
+            forward_next, finish_next = reduction(with_rows(gather, [own_energy]) if it == 0 else gather)
+            for face in range(faces):
+                mz_v[face] = jnp.dot(k_sum[face], half_v[face], preferred_element_type=F32)
+            if it == 0:
+                forward_h()
+            else:
+                rows = finish_h()
+                high, low = split(rows)
+                lane = lax.broadcasted_iota(jnp.int32, (ncq, cols), 1)
+                hess_v[...] = jnp.where(lane < 2 * ncq, high.astype(F32), low.astype(F32)).astype(BF16)
+        coarse = finish()
+        if it == 0:
+            nu0 = coarse[ncoarse : ncoarse + 1]
+            rho0 = coarse[ncoarse + 1 : ncoarse + 2]
+            full = nu0 / rho0
+            scale = full
+            coarse = jnp.where(coarse_row < ncoarse, coarse, 0.0)
+        else:
+            own = coarse[ncoarse : ncoarse + 1]
+            coarse = coarse + jnp.dot(hess_v[...], tall_stack, preferred_element_type=F32)
+            coarse = jnp.where(coarse_row < ncoarse, coarse * scale, 0.0)
+            if it == 1:
+                shrink = (rho0 / nu0) * (rho0 / (own + coarse_energy))
+                scale = full * shrink
+        coarse_energy, stack, tall_stack = solve_coarse(coarse)
+        if not last:
+            for face in range(faces):
+                z = (0.5 * masks[face]) * mz_v[face]
+                z = scale * (z + jnp.dot(lift_v[face], tall_stack, preferred_element_type=F32))
+                flatten(face, z)
+                if face % 2:
+                    z_v[it + 1, face // 2] = z
+            signed_v[...] = zflat[...].astype(BF16)
+            forward, finish = forward_next, finish_next
+    start_eb(finish_ea())
+    for axis in range(3):
+        wait_halo(ITERS - 1, 2 * axis + 1)
+        full_image(ITERS - 1, axis, stack)
+
+    sums = finish_eb()
+    rho, g00, g01, g11, g12, g22 = [sums[index : index + 1] for index in range(6)]
+    g22 = g22 + coarse_energy
+    g02 = shrink * g11
+    b1 = full * g00
+    b2 = full * shrink * g01
+    low1 = g01 / g00
+    low2 = g02 / g00
+    pivot1 = g11 - low1 * g01
+    cross = g12 - low1 * g02
+    low3 = cross / pivot1
+    pivot2 = g22 - low2 * g02 - low3 * cross
+    y1 = b1 - low1 * rho
+    y2 = b2 - low2 * rho - low3 * y1
+    c2 = y2 / pivot2
+    c1 = y1 / pivot1 - low3 * c2
+    c0 = rho / g00 - low1 * c1 - low2 * c2
+    for axis in range(3):
+        mult_ref[axis, :, 0, :] = c0 * z_v[0, axis] + c1 * z_v[1, axis] + c2 * z_v[2, axis]
+        resid_ref[axis, :, 0, :] = res_v[axis] - c0 * v_v[0, axis] - c1 * v_v[1, axis] - c2 * v_v[2, axis]
+
+    for axis in range(3):
+        when_has(2 * axis + 1, lambda axis=axis: rhs_copy(axis).wait_send())
+        when_has(2 * axis + 1, lambda axis=axis: product_copy(axis).wait_send())
+    for face in range(faces):
+        when_has(face, lambda face=face: k_drain(face))
+        when_has(face, lambda face=face: c_copy(face).wait_send())
+        for it in range(ITERS):
+            if it + 1 < ITERS or face % 2 == 0:
+                when_has(face, lambda face=face, it=it: halo_copy(it, face).wait_send())
+    for drain in drains:
+        drain()
+
+
+def kernel_wide(
     sizes,
     dims,
     rhs_hbm,
@@ -435,6 +944,9 @@
     corners = ids.shape[0]
     total = faces * width
     ncq = round_up(ncoarse + 2, 32)
+    narrow = 4 * ncq == cols
+    banks = ITERS + 1 if narrow else 2
+    trips = ITERS + 1 if narrow else ITERS
     wide = round_up(width, 128)
     span = round_up((faces - 1) * width // 128 * 128 + max(round_up(width + 127, 128), wide), 128)
     nx, ny, nz = sizes
@@ -450,7 +962,7 @@
 
     out = jax.ShapeDtypeStruct(rhs.shape, F32)
     mult, resid = pl.pallas_call(
-        functools.partial(kernel, sizes, (faces, width, cols, ncoarse, corners)),
+        functools.partial(kernel if narrow else kernel_wide, sizes, (faces, width, cols, ncoarse, corners)),
         out_shape=(out, out),
         in_specs=[any_space] * 5 + [smem],
         out_specs=(vmem, vmem),
@@ -463,33 +975,54 @@
             pltpu.VMEM(coarse_inverse.shape, BF16),
             pltpu.VMEM((3, width, cols), BF16),
             pltpu.VMEM((3, width, cols), BF16),
+            *(
+                [
+                    pltpu.VMEM(stiffness.shape, BF16),
+                    pltpu.VMEM((2, wide, 128), F32),
+                    pltpu.VMEM((3, width, cols), BF16),
+                    pltpu.VMEM((3, width, cols), BF16),
+                ]
+                if narrow
+                else []
+            ),
             pltpu.VMEM((ncq, span), F32),
             pltpu.VMEM((ncq, total), BF16),
             pltpu.VMEM((faces, ncq, wide), BF16),
             pltpu.VMEM((faces, ncq, wide), BF16),
             pltpu.VMEM((faces, width, (4 if ncq <= 64 else 2) * ncq), BF16),
+            *(
+                [
+                    pltpu.VMEM((faces, 4 * ncq, wide), BF16),
+                    pltpu.VMEM((faces, width, 4 * ncq), BF16),
+                    pltpu.VMEM((ncq, cols), BF16),
+                ]
+                if narrow
+                else []
+            ),
             pltpu.VMEM((3, width, cols), F32),
             pltpu.VMEM((ITERS, 3, width, cols), F32),
             pltpu.VMEM((ITERS, 3, width, cols), F32),
             pltpu.VMEM((faces, width, cols), BF16),
+            *([pltpu.VMEM((faces, width, cols), F32)] if narrow else []),
             pltpu.VMEM((total, cols), F32),
             pltpu.VMEM((total, cols), BF16),
             pltpu.VMEM((total, cols), F32),
             pltpu.VMEM((ITERS, faces, width, cols), BF16),
             pltpu.VMEM((ITERS, faces, width, cols), BF16),
-            pltpu.VMEM((2, plane, ncq, cols), F32),
-            pltpu.VMEM((2, nz, ncq, cols), F32),
+            pltpu.VMEM((banks, plane, ncq, cols), F32),
+            pltpu.VMEM((banks, nz, ncq, cols), F32),
             pltpu.VMEM((1, plane, 8, cols), F32),
             pltpu.VMEM((1, nz, 8, cols), F32),
             dma((5,)),
             dma((3, faces)),
             dma((3, faces)),
+            *([dma((faces, wide // 128)), dma((faces, wide // 128))] if narrow else []),
             dma((ITERS, faces)),
             dma((ITERS, faces)),
-            dma((ITERS, plane)),
-            dma((ITERS, plane)),
-            dma((ITERS, nz)),
-            dma((ITERS, nz)),
+            dma((trips, plane)),
+            dma((trips, plane)),
+            dma((trips, nz)),
+            dma((trips, nz)),
             dma((1, plane)),
             dma((1, plane)),
             dma((1, nz)),

time: 50.4 us -> 48.8 us (0.968)
  Pallas kernels: 49.6 us -> 48 us
    pallas_call x1, Pallas kernels: 48.6 us -> 47.1 us  [body(): pl.pallas_call(functools.partial(kernel if narrow else kernel_wide, sizes...]
where the time goes in v2:
time: 48.8 us; the launch traced here: 48.6 us
  Pallas kernels  48 us (98%)
  between operations  0.64 us (1%)
    pallas_call x1, Pallas kernels, body(): pl.pallas_call(functools.partial(kernel if narrow else kernel_wide, sizes...  47.1 us

profile of v2, /device:TPU:0, one launch (start us, length us, event | category | flops | bytes accessed | tf_op | source)
XLA Modules:
  0.0 48.6 jit_solution(13056527719433126541)
XLA Ops:
  0.6 47.1 %shard_map.77 = (f32[3,300,1,128]{3,2,1,0:T(1,128)S(1)}, f32[3,300,1,128]{3,2,1,0:T(1,128)S(1)}) custom-call(f32[3,300,1,128]{3,2,1,0:T(1,128)} %bitcast.13, bf16[1800,1800]{1,0:T(8,128)(2,1)} %bitcast.11, bf16[24,1800]{1,0:T(8,128)(2,1)} %bitcast.14, bf16[6,300,300]{2,1,0:T(8,128)(2,1)} %bitcast.12, bf16[27,27]{1,0:T(8,128)(2,1)} %cinv_hbm.1, s32[8]{0:T(128)} %bitcast.15), custom_call_target="tpu_custom_call" | custom-call | tf_op jit(solution)/shard_map/pallas_call | solution.py:964
  47.7 0.9 %shard_map.78 = (f32[3,300,1,128]{3,2,1,0:T(1,128)}, f32[3,300,1,128]{3,2,1,0:T(1,128)}) custom-call(f32[3,300,1,128]{3,2,1,0:T(1,128)S(1)} %get-tuple-element.6.mult_ref, f32[3,300,1,128]{3,2,1,0:T(1,128)S(1)} %get-tuple-element.7.resid_ref), custom_call_target="tpu_custom_call" | custom-call | tf_op jit(solution)/shard_map/pallas_call | solution.py:1035

commit v3 on v2

--- a/solution.py
+++ b/solution.py
@@ -64,6 +64,7 @@
     energy_a,
     energy_b,
     local_sem,
+    rhs_sem,
     setup_send,
     setup_recv,
     k_send,
@@ -78,6 +79,10 @@
     ea_recv,
     eb_send,
     eb_recv,
+    late_v,
+    late_send,
+    late_recv,
+    ring_sem,
 ):
     nx, ny, nz = sizes
     faces, width, cols, ncoarse, corners = dims
@@ -107,25 +112,43 @@
         return {"gz": lax.rem(here[2] + offset, nz)}
 
     barrier = pltpu.get_barrier_semaphore()
-    for offset in range(1, plane):
-        pl.semaphore_signal(barrier, inc=1, device_id=plane_peer(offset), device_id_type=MESH)
-    for offset in range(1, nz):
-        pl.semaphore_signal(barrier, inc=1, device_id=z_peer(offset), device_id_type=MESH)
-
-    loads = []
+    around = sum(jnp.where(flag, 1, 0) for flag in has)
+
+    def greet(semaphore):
+        for face in range(faces):
+
+            @pl.when(has[face])
+            def _(face=face):
+                pl.semaphore_signal(semaphore, inc=1, device_id=neighbour(face), device_id_type=MESH)
+
+    greet(barrier)
+    levels = ring_sem.shape[0]
+
+    loads = [None]
+    rhs_loads = [
+        pltpu.make_async_copy(rhs_hbm.at[axis, :, 0, :], rhs_v.at[axis], rhs_sem.at[axis]) for axis in range(3)
+    ]
+    for copy in rhs_loads:
+        copy.start()
     for index, (src, dst) in enumerate(
-        ((rhs_hbm, rhs_v), (coup_hbm, coup_v), (cinv_hbm, cinv_v), (stiff_hbm, k_own), (flex_hbm, flex_v))
+        ((coup_hbm, coup_v), (cinv_hbm, cinv_v), (stiff_hbm, k_own), (flex_hbm, flex_v))
     ):
         copy = pltpu.make_async_copy(src, dst, local_sem.at[index])
         copy.start()
         loads.append(copy)
 
-    loads[0].wait()
-    for axis in range(3):
-        owned = rhs_v[axis, :, 0, :] * masks[2 * axis + 1]
+    for axis in (2, 0, 1):
+        rhs_loads[axis].wait()
+        owned = rhs_v[axis] * masks[2 * axis + 1]
         res_v[axis] = owned
         r_send[axis] = owned.astype(BF16)
-    pl.semaphore_wait(barrier, plane - 1 + nz - 1)
+    pl.semaphore_wait(barrier, around)
+    greet(ring_sem.at[0])
+
+    def widen(level):
+        pl.semaphore_wait(ring_sem.at[level], around)
+        if level + 1 < levels:
+            greet(ring_sem.at[level + 1])
 
     def remote(src, dst, send_sem, recv_sem, target):
         return pltpu.make_async_remote_copy(
@@ -195,6 +218,8 @@
         product = jnp.dot(k_own[face], half, preferred_element_type=F32) * (0.5 * masks[face])
         p_send[axis] = product.astype(BF16)
         when_has(face, lambda axis=axis: product_copy(axis).start())
+    for level in range(1):
+        widen(level)
 
     for face in range(faces):
 
@@ -239,6 +264,8 @@
         when_has(face, lambda face=face: c_copy(face).start())
     for face in (5, 1, 3):
         when_has(face, lambda face=face: k_start(face))
+    for level in range(1, min(levels, 2)):
+        widen(level)
     k_pad[...] = jnp.zeros(k_pad.shape, F32)
 
     loads[2].wait()
@@ -275,8 +302,7 @@
         return start, finish, drain
 
     coarse_row = lax.broadcasted_iota(jnp.int32, (ncq, cols), 0)
-    scalar_row = lax.broadcasted_iota(jnp.int32, (8, cols), 0)
-    moments = []
+    lane_group = lax.broadcasted_iota(jnp.int32, (8, cols), 1) // ncq
     drains = []
     rounds = []
 
@@ -289,6 +315,29 @@
         start_a(value)
         return lambda: start_b(finish_a()), finish_b
 
+    everyone = [(p, z) for z in reversed(range(nz)) for p in reversed(range(plane)) if p + z > 0]
+    me_all = me_plane * nz + here[2]
+
+    def late_copy(p, z, slot):
+        target = dict(plane_peer(p), **z_peer(z))
+        index = p * nz + z
+        return remote(late_v.at[slot], late_v.at[slot], late_send.at[index], late_recv.at[index], target)
+
+    def start_late(value):
+        late_v[me_all] = value
+        for p, z in everyone:
+            late_copy(p, z, me_all).start()
+
+    def finish_late():
+        for p, z in everyone:
+            source = lax.rem(me_plane + plane - p, plane) * nz + lax.rem(here[2] + nz - z, nz)
+            late_copy(p, z, source).wait_recv()
+        return jnp.sum(late_v[...], axis=0)
+
+    def drain_late():
+        for p, z in everyone:
+            late_copy(p, z, me_all).wait_send()
+
     def with_rows(value, rows_out):
         for index, row in enumerate(rows_out):
             value = jnp.where(coarse_row == ncoarse + index, row, value)
@@ -322,7 +371,7 @@
             sol = jnp.concatenate([sol, jnp.zeros((ncq - ncoarse, cols), F32)], axis=0)
         high, low = split(sol)
         return (
-            total_of(rhs * sol),
+            sol,
             jnp.concatenate([high, high, low, low], axis=0),
             jnp.concatenate([high, low, high, low], axis=0),
         )
@@ -368,6 +417,8 @@
         when_has(face, lambda axis=axis: rhs_copy(axis).wait_recv())
         half = (-0.5 * r_recv[axis].astype(F32)).astype(BF16)
         mz_v[face] = jnp.dot(k_own[face], half, preferred_element_type=F32) * (0.5 * masks[face])
+    for level in range(2, levels):
+        widen(level)
     for axis in (2, 0, 1):
         face = 2 * axis + 1
         add_stiffness(face)
@@ -382,7 +433,6 @@
         face = 2 * axis
         when_has(face, lambda axis=axis: product_copy(axis).wait_recv())
         flatten(face, mz_v[face] - p_recv[axis].astype(F32))
-    moments.append(rho_acc)
     signed = zflat[...].astype(BF16)
     signed_v[...] = signed
     part = jnp.dot(casm_v[...], signed, preferred_element_type=F32)
@@ -395,10 +445,12 @@
     scale = None
     shrink = None
     stack = None
+    sol = None
+    rhs_parts = []
     for it in range(ITERS):
         last = it + 1 == ITERS
         energy_acc = jnp.zeros((8, cols), F32)
-        dots = [jnp.zeros((1, cols), F32) for _ in range(it + 1)]
+        mixed = jnp.zeros((1, cols), F32)
         for position, axis in enumerate(order):
             begin, end = cuts[axis], cuts[axis + 1]
             image = jnp.dot(flex_v[begin:end, :], signed_v[...], preferred_element_type=F32)
@@ -409,15 +461,17 @@
             for face in (2 * axis, 2 * axis + 1):
                 img_send[it, face] = imgflat[face * width : (face + 1) * width, :].astype(BF16)
             if it > 0:
-                whole = full_image(it - 1, axis, stack)
-                for index in range(it + 1):
-                    if index < it or last:
-                        dots[index] = dots[index] + total_of(z_v[index, axis] * whole)
+                full_image(it - 1, axis, stack)
+                if last:
+                    jump = local_jump(it - 1, 2 * axis + 1) * masks[2 * axis + 1]
+                    mixed = mixed + total_of(z_v[it, axis] * jump)
             for face in (2 * axis, 2 * axis + 1):
                 if not last or face % 2 == 0:
                     when_has(face, lambda face=face, it=it: halo_copy(it, face).start())
-        if it > 0:
-            moments.extend(dots if last else dots[0:it])
+        if last:
+            energy = total_of(energy_acc)
+            late_row = lax.broadcasted_iota(jnp.int32, (2, cols), 0)
+            start_late(jnp.where(late_row == 0, mixed, energy))
         if it == 0:
             hess = jnp.zeros((ncq, cols), F32)
             for axis in order:
@@ -426,21 +480,18 @@
             for axis in order:
                 add_stiffness(2 * axis)
                 prepare(2 * axis)
-            forward_h, finish_h = reduction(hess)
-        else:
-            forward()
-        if last:
-            moments.append(total_of(energy_acc))
-            block = jnp.zeros((8, cols), F32)
-            for index, row in enumerate(moments):
-                block = jnp.where(scalar_row == index, row, block)
+            packed = jnp.zeros((8, cols), F32)
+            for group in range(ncq // 8):
+                packed = jnp.where(lane_group == group, hess[8 * group : 8 * group + 8], packed)
             start_ea, finish_ea, drain_ea = exchange(energy_a, 0, me_plane, plane, plane_peer, ea_send, ea_recv)
             start_eb, finish_eb, drain_eb = exchange(energy_b, 0, here[2], nz, z_peer, eb_send, eb_recv)
             drains.extend((drain_ea, drain_eb))
-            start_ea(block)
+            start_ea(packed)
         else:
+            forward()
+        if not last:
             gather = jnp.zeros((2 * ncq, cols), F32)
-            own_energy = jnp.zeros((1, cols), F32)
+            products = [jnp.zeros((1, cols), F32) for _ in range(it + 1)]
             for axis in order:
                 for face in (2 * axis, 2 * axis + 1):
                     wait_halo(it, face)
@@ -451,17 +502,23 @@
                         gather = gather + jnp.dot(
                             span_v[face, ncq : 3 * ncq, 0:width], half, preferred_element_type=F32
                         )
-                        if it == 0:
-                            own_energy = own_energy + total_of(z_v[0, axis] * jump * masks[face])
+                        jump = jump * masks[face]
+                        for index in range(it + 1):
+                            products[index] = products[index] + total_of(z_v[index, axis] * jump)
             gather = 2.0 * (gather[0:ncq] + gather[ncq : 2 * ncq])
-            forward_next, finish_next = reduction(with_rows(gather, [own_energy]) if it == 0 else gather)
+            forward_next, finish_next = reduction(with_rows(gather, products))
             for face in range(faces):
                 mz_v[face] = jnp.dot(k_sum[face], half_v[face], preferred_element_type=F32)
             if it == 0:
-                forward_h()
+                start_eb(finish_ea())
             else:
-                rows = finish_h()
-                high, low = split(rows)
+                packed = finish_eb()
+                groups = []
+                for group in range(ncq // 8):
+                    piece = jnp.where(lane_group == group, packed, 0.0)
+                    piece = piece + pltpu.roll(piece, 2 * ncq, 1)
+                    groups.append(piece + pltpu.roll(piece, ncq, 1))
+                high, low = split(jnp.concatenate(groups, axis=0))
                 lane = lax.broadcasted_iota(jnp.int32, (ncq, cols), 1)
                 hess_v[...] = jnp.where(lane < 2 * ncq, high.astype(F32), low.astype(F32)).astype(BF16)
         coarse = finish()
@@ -472,13 +529,19 @@
             scale = full
             coarse = jnp.where(coarse_row < ncoarse, coarse, 0.0)
         else:
-            own = coarse[ncoarse : ncoarse + 1]
+            sums = [coarse[ncoarse + index : ncoarse + index + 1] for index in range(it)]
             coarse = coarse + jnp.dot(hess_v[...], tall_stack, preferred_element_type=F32)
             coarse = jnp.where(coarse_row < ncoarse, coarse * scale, 0.0)
             if it == 1:
-                shrink = (rho0 / nu0) * (rho0 / (own + coarse_energy))
+                g00 = sums[0] + total_of(rhs_parts[0] * sol)
+                shrink = (rho0 / nu0) * (rho0 / g00)
                 scale = full * shrink
-        coarse_energy, stack, tall_stack = solve_coarse(coarse)
+        rhs_parts.append(coarse)
+        if last:
+            g01 = sums[0] + total_of(rhs_parts[0] * sol)
+            g11 = sums[1] + total_of(rhs_parts[1] * sol)
+            coarse12 = total_of(coarse * sol)
+        sol, stack, tall_stack = solve_coarse(coarse)
         if not last:
             for face in range(faces):
                 z = (0.5 * masks[face]) * mz_v[face]
@@ -488,14 +551,15 @@
                     z_v[it + 1, face // 2] = z
             signed_v[...] = zflat[...].astype(BF16)
             forward, finish = forward_next, finish_next
-    start_eb(finish_ea())
     for axis in range(3):
         wait_halo(ITERS - 1, 2 * axis + 1)
         full_image(ITERS - 1, axis, stack)
 
-    sums = finish_eb()
-    rho, g00, g01, g11, g12, g22 = [sums[index : index + 1] for index in range(6)]
-    g22 = g22 + coarse_energy
+    late = finish_late()
+    drains.append(drain_late)
+    rho = rho0
+    g12 = late[0:1] + coarse12
+    g22 = late[1:2] + total_of(coarse * sol)
     g02 = shrink * g11
     b1 = full * g00
     b2 = full * shrink * g01
@@ -511,8 +575,8 @@
     c1 = y1 / pivot1 - low3 * c2
     c0 = rho / g00 - low1 * c1 - low2 * c2
     for axis in range(3):
-        mult_ref[axis, :, 0, :] = c0 * z_v[0, axis] + c1 * z_v[1, axis] + c2 * z_v[2, axis]
-        resid_ref[axis, :, 0, :] = res_v[axis] - c0 * v_v[0, axis] - c1 * v_v[1, axis] - c2 * v_v[2, axis]
+        mult_ref[axis] = c0 * z_v[0, axis] + c1 * z_v[1, axis] + c2 * z_v[2, axis]
+        resid_ref[axis] = res_v[axis] - c0 * v_v[0, axis] - c1 * v_v[1, axis] - c2 * v_v[2, axis]
 
     for axis in range(3):
         when_has(2 * axis + 1, lambda axis=axis: rhs_copy(axis).wait_send())
@@ -922,10 +986,13 @@
 
 
 def store(mult_ref, resid_ref, mult_hbm, resid_hbm, sem):
-    copies = (
-        pltpu.make_async_copy(mult_ref, mult_hbm, sem.at[0]),
-        pltpu.make_async_copy(resid_ref, resid_hbm, sem.at[1]),
-    )
+    copies = [
+        pltpu.make_async_copy(src.at[axis], dst.at[axis, :, 0, :], sem.at[index, axis])
+        if len(src.shape) == 3
+        else pltpu.make_async_copy(src.at[axis], dst.at[axis], sem.at[index, axis])
+        for axis in range(mult_ref.shape[0])
+        for index, (src, dst) in enumerate(((mult_ref, mult_hbm), (resid_ref, resid_hbm)))
+    ]
     for copy in copies:
         copy.start()
     for copy in copies:
@@ -944,9 +1011,8 @@
     corners = ids.shape[0]
     total = faces * width
     ncq = round_up(ncoarse + 2, 32)
-    narrow = 4 * ncq == cols
-    banks = ITERS + 1 if narrow else 2
-    trips = ITERS + 1 if narrow else ITERS
+    narrow = 4 * ncq == cols and 32 * ncq == 8 * cols
+    banks = ITERS if narrow else 2
     wide = round_up(width, 128)
     span = round_up((faces - 1) * width // 128 * 128 + max(round_up(width + 127, 128), wide), 128)
     nx, ny, nz = sizes
@@ -961,13 +1027,14 @@
         return pltpu.with_memory_space_constraint(operand, pltpu.HBM)
 
     out = jax.ShapeDtypeStruct(rhs.shape, F32)
+    tiled = jax.ShapeDtypeStruct((3, width, cols), F32)
     mult, resid = pl.pallas_call(
         functools.partial(kernel if narrow else kernel_wide, sizes, (faces, width, cols, ncoarse, corners)),
-        out_shape=(out, out),
+        out_shape=(tiled, tiled) if narrow else (out, out),
         in_specs=[any_space] * 5 + [smem],
         out_specs=(vmem, vmem),
         scratch_shapes=[
-            pltpu.VMEM(rhs.shape, F32),
+            pltpu.VMEM(tiled.shape if narrow else rhs.shape, F32),
             pltpu.VMEM(flex.shape, BF16),
             pltpu.VMEM(coupling.shape, BF16),
             pltpu.VMEM(stiffness.shape, BF16),
@@ -1014,19 +1081,30 @@
             pltpu.VMEM((1, plane, 8, cols), F32),
             pltpu.VMEM((1, nz, 8, cols), F32),
             dma((5,)),
+            *([dma((3,))] if narrow else []),
             dma((3, faces)),
             dma((3, faces)),
             *([dma((faces, wide // 128)), dma((faces, wide // 128))] if narrow else []),
             dma((ITERS, faces)),
             dma((ITERS, faces)),
-            dma((trips, plane)),
-            dma((trips, plane)),
-            dma((trips, nz)),
-            dma((trips, nz)),
+            dma((ITERS, plane)),
+            dma((ITERS, plane)),
+            dma((ITERS, nz)),
+            dma((ITERS, nz)),
             dma((1, plane)),
             dma((1, plane)),
             dma((1, nz)),
             dma((1, nz)),
+            *(
+                [
+                    pltpu.VMEM((plane * nz, 2, cols), F32),
+                    dma((plane * nz,)),
+                    dma((plane * nz,)),
+                    pltpu.SemaphoreType.REGULAR((max(nx + ny - 2, nz - 1, 2) - 1,)),
+                ]
+                if narrow
+                else []
+            ),
         ],
         compiler_params=pltpu.CompilerParams(
             collective_id=0, has_side_effects=True, vmem_limit_bytes=(28 if ncq <= 64 else 54) * 1024 * 1024
@@ -1037,7 +1115,7 @@
         out_shape=(out, out),
         in_specs=[vmem, vmem],
         out_specs=(hbm, hbm),
-        scratch_shapes=[dma((2,))],
+        scratch_shapes=[dma((2, 3))],
         compiler_params=pltpu.CompilerParams(vmem_limit_bytes=1024 * 1024),
     )(mult, resid)
     return (mult.reshape(dual_rhs.shape), resid.reshape(dual_rhs.shape))

time: 48.8 us -> 45.2 us (0.926)
  Pallas kernels: 48 us -> 44 us
    pallas_call x1, Pallas kernels: 47.1 us -> 43.1 us  [body(): pl.pallas_call(functools.partial(kernel if narrow else kernel_wide, sizes...]
where the time goes in v3:
time: 45.2 us; the launch traced here: 44.7 us
  Pallas kernels  44 us (97%)
  between operations  0.64 us (1%)
    pallas_call x1, Pallas kernels, body(): pl.pallas_call(functools.partial(kernel if narrow else kernel_wide, sizes...  43.1 us
    pallas_call x1, Pallas kernels, body(): pl.pallas_call(store, out_shape=(out, out), in_specs=[vmem, vmem], out_sp...  0.97 us

profile of v3, /device:TPU:0, one launch (start us, length us, event | category | flops | bytes accessed | tf_op | source)
XLA Modules:
  0.0 44.7 jit_solution(15268055589585357164)
XLA Ops:
  0.6 43.1 %shard_map.77 = (f32[3,300,128]{2,1,0:T(8,128)S(1)}, f32[3,300,128]{2,1,0:T(8,128)S(1)}) custom-call(f32[3,300,1,128]{3,2,1,0:T(1,128)} %bitcast.13, bf16[1800,1800]{1,0:T(8,128)(2,1)} %bitcast.11, bf16[24,1800]{1,0:T(8,128)(2,1)} %bitcast.14, bf16[6,300,300]{2,1,0:T(8,128)(2,1)} %bitcast.12, bf16[27,27]{1,0:T(8,128)(2,1)} %cinv_hbm.1, s32[8]{0:T(128)} %bitcast.15), custom_call_target="tpu_custom_call" | custom-call | tf_op jit(solution)/shard_map/pallas_call | solution.py:1031
  43.7 1.0 %shard_map.78 = (f32[3,300,1,128]{3,2,1,0:T(1,128)}, f32[3,300,1,128]{3,2,1,0:T(1,128)}) custom-call(f32[3,300,128]{2,1,0:T(8,128)S(1)} %get-tuple-element.6.mult_ref, f32[3,300,128]{2,1,0:T(8,128)S(1)} %get-tuple-element.7.resid_ref), custom_call_target="tpu_custom_call" | custom-call | tf_op jit(solution)/shard_map/pallas_call | solution.py:1113

commit v4 on v3

--- a/solution.py
+++ b/solution.py
@@ -391,9 +391,7 @@
         lift_v[face] = span_v[face].astype(F32).T[0:width].astype(BF16)
         if face % 2 == 0:
             return None
-        product = lax.dot_general(
-            both[:, 0:width], tall, (((1,), (1,)), ((), ())), preferred_element_type=F32
-        )
+        product = jnp.dot(both[:, 0:width], lift_v[face], preferred_element_type=F32)
         product = product[0:ncq] + product[ncq : 2 * ncq]
         return product + pltpu.roll(product, 2 * ncq, 1)
 
@@ -446,6 +444,7 @@
     shrink = None
     stack = None
     sol = None
+    tall_stack = full = rho0 = nu0 = g00 = g01 = g11 = coarse12 = None
     rhs_parts = []
     for it in range(ITERS):
         last = it + 1 == ITERS
@@ -474,9 +473,10 @@
             start_late(jnp.where(late_row == 0, mixed, energy))
         if it == 0:
             hess = jnp.zeros((ncq, cols), F32)
-            for axis in order:
+            hess = hess + prepare(2 * order[0] + 1)
+            forward()
+            for axis in order[1:]:
                 hess = hess + prepare(2 * axis + 1)
-            forward()
             for axis in order:
                 add_stiffness(2 * axis)
                 prepare(2 * axis)
@@ -488,30 +488,12 @@
             drains.extend((drain_ea, drain_eb))
             start_ea(packed)
         else:
+            if it == 1:
+                start_eb(finish_ea())
             forward()
-        if not last:
-            gather = jnp.zeros((2 * ncq, cols), F32)
-            products = [jnp.zeros((1, cols), F32) for _ in range(it + 1)]
-            for axis in order:
-                for face in (2 * axis, 2 * axis + 1):
-                    wait_halo(it, face)
-                    jump = local_jump(it, face)
-                    half = (0.5 * jump).astype(BF16)
-                    half_v[face] = half
-                    if face % 2:
-                        gather = gather + jnp.dot(
-                            span_v[face, ncq : 3 * ncq, 0:width], half, preferred_element_type=F32
-                        )
-                        jump = jump * masks[face]
-                        for index in range(it + 1):
-                            products[index] = products[index] + total_of(z_v[index, axis] * jump)
-            gather = 2.0 * (gather[0:ncq] + gather[ncq : 2 * ncq])
-            forward_next, finish_next = reduction(with_rows(gather, products))
-            for face in range(faces):
-                mz_v[face] = jnp.dot(k_sum[face], half_v[face], preferred_element_type=F32)
-            if it == 0:
-                start_eb(finish_ea())
-            else:
+        def coarse_step():
+            nonlocal sol, stack, tall_stack, scale, shrink, full, rho0, nu0, g00, g01, g11, coarse12
+            if it == 1:
                 packed = finish_eb()
                 groups = []
                 for group in range(ncq // 8):
@@ -521,36 +503,66 @@
                 high, low = split(jnp.concatenate(groups, axis=0))
                 lane = lax.broadcasted_iota(jnp.int32, (ncq, cols), 1)
                 hess_v[...] = jnp.where(lane < 2 * ncq, high.astype(F32), low.astype(F32)).astype(BF16)
-        coarse = finish()
-        if it == 0:
-            nu0 = coarse[ncoarse : ncoarse + 1]
-            rho0 = coarse[ncoarse + 1 : ncoarse + 2]
-            full = nu0 / rho0
-            scale = full
-            coarse = jnp.where(coarse_row < ncoarse, coarse, 0.0)
-        else:
-            sums = [coarse[ncoarse + index : ncoarse + index + 1] for index in range(it)]
-            coarse = coarse + jnp.dot(hess_v[...], tall_stack, preferred_element_type=F32)
-            coarse = jnp.where(coarse_row < ncoarse, coarse * scale, 0.0)
-            if it == 1:
-                g00 = sums[0] + total_of(rhs_parts[0] * sol)
-                shrink = (rho0 / nu0) * (rho0 / g00)
-                scale = full * shrink
-        rhs_parts.append(coarse)
+            coarse = finish()
+            if it == 0:
+                nu0 = coarse[ncoarse : ncoarse + 1]
+                rho0 = coarse[ncoarse + 1 : ncoarse + 2]
+                full = nu0 / rho0
+                scale = full
+                coarse = jnp.where(coarse_row < ncoarse, coarse, 0.0)
+            else:
+                sums = [coarse[ncoarse + index : ncoarse + index + 1] for index in range(it)]
+                coarse = coarse + jnp.dot(hess_v[...], tall_stack, preferred_element_type=F32)
+                coarse = jnp.where(coarse_row < ncoarse, coarse * scale, 0.0)
+                if it == 1:
+                    g00 = sums[0] + total_of(rhs_parts[0] * sol)
+                    shrink = (rho0 / nu0) * (rho0 / g00)
+                    scale = full * shrink
+            rhs_parts.append(coarse)
+            if last:
+                g01 = sums[0] + total_of(rhs_parts[0] * sol)
+                g11 = sums[1] + total_of(rhs_parts[1] * sol)
+                coarse12 = total_of(coarse * sol)
+            sol, stack, tall_stack = solve_coarse(coarse)
+
+        def settle(face):
+            z = (0.5 * masks[face]) * mz_v[face]
+            z = scale * (z + jnp.dot(lift_v[face], tall_stack, preferred_element_type=F32))
+            flatten(face, z)
+            if face % 2:
+                z_v[it + 1, face // 2] = z
+
         if last:
-            g01 = sums[0] + total_of(rhs_parts[0] * sol)
-            g11 = sums[1] + total_of(rhs_parts[1] * sol)
-            coarse12 = total_of(coarse * sol)
-        sol, stack, tall_stack = solve_coarse(coarse)
-        if not last:
-            for face in range(faces):
-                z = (0.5 * masks[face]) * mz_v[face]
-                z = scale * (z + jnp.dot(lift_v[face], tall_stack, preferred_element_type=F32))
-                flatten(face, z)
+            coarse_step()
+            continue
+        gather = jnp.zeros((2 * ncq, cols), F32)
+        products = [jnp.zeros((1, cols), F32) for _ in range(it + 1)]
+        for position, axis in enumerate(order):
+            for face in (2 * axis, 2 * axis + 1):
+                wait_halo(it, face)
+                jump = local_jump(it, face)
+                half = (0.5 * jump).astype(BF16)
+                half_v[face] = half
                 if face % 2:
-                    z_v[it + 1, face // 2] = z
-            signed_v[...] = zflat[...].astype(BF16)
-            forward, finish = forward_next, finish_next
+                    gather = gather + jnp.dot(
+                        span_v[face, ncq : 3 * ncq, 0:width], half, preferred_element_type=F32
+                    )
+                    jump = jump * masks[face]
+                    for index in range(it + 1):
+                        products[index] = products[index] + total_of(z_v[index, axis] * jump)
+            if position + 1 < len(order):
+                for face in (2 * axis, 2 * axis + 1):
+                    mz_v[face] = jnp.dot(k_sum[face], half_v[face], preferred_element_type=F32)
+        gather = 2.0 * (gather[0:ncq] + gather[ncq : 2 * ncq])
+        forward_next, finish_next = reduction(with_rows(gather, products))
+        axis = order[-1]
+        for face in (2 * axis, 2 * axis + 1):
+            mz_v[face] = jnp.dot(k_sum[face], half_v[face], preferred_element_type=F32)
+        coarse_step()
+        for face in range(faces):
+            settle(face)
+        signed_v[...] = zflat[...].astype(BF16)
+        forward, finish = forward_next, finish_next
     for axis in range(3):
         wait_halo(ITERS - 1, 2 * axis + 1)
         full_image(ITERS - 1, axis, stack)
@@ -559,7 +571,7 @@
     drains.append(drain_late)
     rho = rho0
     g12 = late[0:1] + coarse12
-    g22 = late[1:2] + total_of(coarse * sol)
+    g22 = late[1:2] + total_of(rhs_parts[2] * sol)
     g02 = shrink * g11
     b1 = full * g00
     b2 = full * shrink * g01
@@ -1011,7 +1023,7 @@
     corners = ids.shape[0]
     total = faces * width
     ncq = round_up(ncoarse + 2, 32)
-    narrow = 4 * ncq == cols and 32 * ncq == 8 * cols
+    narrow = 4 * ncq == cols and ncq == 32
     banks = ITERS if narrow else 2
     wide = round_up(width, 128)
     span = round_up((faces - 1) * width // 128 * 128 + max(round_up(width + 127, 128), wide), 128)

time: 45.2 us -> 43.3 us (0.958)
  Pallas kernels: 44 us -> 42.5 us
    pallas_call x1, Pallas kernels: 43.1 us -> 41.5 us  [body(): pl.pallas_call(functools.partial(kernel if narrow else kernel_wide, sizes...]
where the time goes in v4:
time: 43.3 us; the launch traced here: 43.1 us
  Pallas kernels  42.5 us (98%)
  between operations  0.64 us (1%)
    pallas_call x1, Pallas kernels, body(): pl.pallas_call(functools.partial(kernel if narrow else kernel_wide, sizes...  41.5 us
    pallas_call x1, Pallas kernels, body(): pl.pallas_call(store, out_shape=(out, out), in_specs=[vmem, vmem], out_sp...  0.97 us

profile of v4, /device:TPU:0, one launch (start us, length us, event | category | flops | bytes accessed | tf_op | source)
XLA Modules:
  0.0 43.1 jit_solution(3802126281599490235)
XLA Ops:
  0.6 41.5 %shard_map.77 = (f32[3,300,128]{2,1,0:T(8,128)S(1)}, f32[3,300,128]{2,1,0:T(8,128)S(1)}) custom-call(f32[3,300,1,128]{3,2,1,0:T(1,128)} %bitcast.13, bf16[1800,1800]{1,0:T(8,128)(2,1)} %bitcast.11, bf16[24,1800]{1,0:T(8,128)(2,1)} %bitcast.14, bf16[6,300,300]{2,1,0:T(8,128)(2,1)} %bitcast.12, bf16[27,27]{1,0:T(8,128)(2,1)} %cinv_hbm.1, s32[8]{0:T(128)} %bitcast.15), custom_call_target="tpu_custom_call" | custom-call | tf_op jit(solution)/shard_map/pallas_call | solution.py:1043
  42.1 1.0 %shard_map.78 = (f32[3,300,1,128]{3,2,1,0:T(1,128)}, f32[3,300,1,128]{3,2,1,0:T(1,128)}) custom-call(f32[3,300,128]{2,1,0:T(8,128)S(1)} %get-tuple-element.6.mult_ref, f32[3,300,128]{2,1,0:T(8,128)S(1)} %get-tuple-element.7.resid_ref), custom_call_target="tpu_custom_call" | custom-call | tf_op jit(solution)/shard_map/pallas_call | solution.py:1125

commit v5 on v4

--- a/solution.py
+++ b/solution.py
@@ -83,6 +83,7 @@
     late_send,
     late_recv,
     ring_sem,
+    energy_v,
 ):
     nx, ny, nz = sizes
     faces, width, cols, ncoarse, corners = dims
@@ -137,6 +138,26 @@
         copy.start()
         loads.append(copy)
 
+    for face in range(faces):
+
+        @pl.when(jnp.logical_not(has[face]))
+        def _(face=face):
+            k_nb[face] = jnp.zeros(k_nb.shape[1:], BF16)
+            c_nb[face] = jnp.zeros(c_nb.shape[1:], BF16)
+            for it in range(ITERS):
+                img_recv[it, face] = jnp.zeros((width, cols), BF16)
+                if sizes[face // 2] == 2:
+                    img_send[it, face] = jnp.zeros((width, cols), BF16)
+                    if face % 2:
+                        z_v[it, face // 2] = jnp.zeros((width, cols), F32)
+
+    for axis in range(3):
+
+        @pl.when(jnp.logical_not(has[2 * axis]))
+        def _(axis=axis):
+            r_recv[axis] = jnp.zeros((width, cols), BF16)
+            p_recv[axis] = jnp.zeros((width, cols), BF16)
+
     for axis in (2, 0, 1):
         rhs_loads[axis].wait()
         owned = rhs_v[axis] * masks[2 * axis + 1]
@@ -220,22 +241,6 @@
         when_has(face, lambda axis=axis: product_copy(axis).start())
     for level in range(1):
         widen(level)
-
-    for face in range(faces):
-
-        @pl.when(jnp.logical_not(has[face]))
-        def _(face=face):
-            k_nb[face] = jnp.zeros(k_nb.shape[1:], BF16)
-            c_nb[face] = jnp.zeros(c_nb.shape[1:], BF16)
-            for it in range(ITERS):
-                img_recv[it, face] = jnp.zeros((width, cols), BF16)
-
-    for axis in range(3):
-
-        @pl.when(jnp.logical_not(has[2 * axis]))
-        def _(axis=axis):
-            r_recv[axis] = jnp.zeros((width, cols), BF16)
-            p_recv[axis] = jnp.zeros((width, cols), BF16)
 
     loads[1].wait()
     lane = lax.broadcasted_iota(jnp.int32, (1, 3 * corners), 1)
@@ -437,7 +442,8 @@
     forward, finish = reduction(with_rows(part, [nu_acc, rho_acc]))
     loads[4].wait()
 
-    cuts = [0] + [round_up(2 * a * width, 16) for a in range(1, faces // 2)] + [total]
+    halves = [extent == 2 for extent in sizes]
+    cuts = [0] + [round_up(2 * a * width - 15 * halves[a - 1], 16) for a in range(1, faces // 2)] + [total]
     order = [faces // 2 - 1] + list(range(faces // 2 - 1))
     span_v[:, :, width:] = jnp.zeros((faces, 4 * ncq, wide - width), BF16)
     scale = None
@@ -452,20 +458,48 @@
         mixed = jnp.zeros((1, cols), F32)
         for position, axis in enumerate(order):
             begin, end = cuts[axis], cuts[axis + 1]
-            image = jnp.dot(flex_v[begin:end, :], signed_v[...], preferred_element_type=F32)
-            imgflat[begin:end, :] = image
-            if last:
-                weighted = image * signed_v[begin:end, :].astype(F32)
-                energy_acc = energy_acc + jnp.sum(weighted.reshape(-1, 8, cols), axis=0)
-            for face in (2 * axis, 2 * axis + 1):
+
+            def solve_rows(low, high, stop):
+                image = jnp.dot(flex_v[low:high, :], signed_v[...], preferred_element_type=F32)
+                imgflat[low:high, :] = image
+                if not last:
+                    return None
+                weighted = image[0 : stop - low] * signed_v[low:stop, :].astype(F32)
+                return jnp.sum(weighted.reshape(-1, 8, cols), axis=0)
+
+            def pack(face):
                 img_send[it, face] = imgflat[face * width : (face + 1) * width, :].astype(BF16)
+
+            if halves[axis]:
+                middle = (2 * axis + 1) * width
+                reach = min(round_up(middle + width, 16), total)
+                spans = ((begin, round_up(middle, 16), round_up(middle, 16)), (middle // 16 * 16, reach, end))
+                for face, (low, high, stop) in zip((2 * axis, 2 * axis + 1), spans):
+
+                    @pl.when(has[face])
+                    def _(face=face, low=low, high=high, stop=stop):
+                        piece = solve_rows(low, high, stop)
+                        if last:
+                            energy_v[...] = piece
+                        pack(face)
+                        if not last or face % 2 == 0:
+                            halo_copy(it, face).start()
+
+                if last:
+                    energy_acc = energy_acc + energy_v[...]
+            else:
+                piece = solve_rows(begin, end, end)
+                if last:
+                    energy_acc = energy_acc + piece
+                for face in (2 * axis, 2 * axis + 1):
+                    pack(face)
             if it > 0:
                 full_image(it - 1, axis, stack)
                 if last:
                     jump = local_jump(it - 1, 2 * axis + 1) * masks[2 * axis + 1]
                     mixed = mixed + total_of(z_v[it, axis] * jump)
             for face in (2 * axis, 2 * axis + 1):
-                if not last or face % 2 == 0:
+                if not halves[axis] and (not last or face % 2 == 0):
                     when_has(face, lambda face=face, it=it: halo_copy(it, face).start())
         if last:
             energy = total_of(energy_acc)
@@ -525,6 +559,15 @@
                 coarse12 = total_of(coarse * sol)
             sol, stack, tall_stack = solve_coarse(coarse)
 
+        def present(face, action):
+            if halves[face // 2]:
+                when_has(face, action)
+            else:
+                action()
+
+        def stiffen(face):
+            mz_v[face] = jnp.dot(k_sum[face], half_v[face], preferred_element_type=F32)
+
         def settle(face):
             z = (0.5 * masks[face]) * mz_v[face]
             z = scale * (z + jnp.dot(lift_v[face], tall_stack, preferred_element_type=F32))
@@ -552,15 +595,15 @@
                         products[index] = products[index] + total_of(z_v[index, axis] * jump)
             if position + 1 < len(order):
                 for face in (2 * axis, 2 * axis + 1):
-                    mz_v[face] = jnp.dot(k_sum[face], half_v[face], preferred_element_type=F32)
+                    present(face, lambda: stiffen(face))
         gather = 2.0 * (gather[0:ncq] + gather[ncq : 2 * ncq])
         forward_next, finish_next = reduction(with_rows(gather, products))
         axis = order[-1]
         for face in (2 * axis, 2 * axis + 1):
-            mz_v[face] = jnp.dot(k_sum[face], half_v[face], preferred_element_type=F32)
+            present(face, lambda: stiffen(face))
         coarse_step()
         for face in range(faces):
-            settle(face)
+            present(face, lambda: settle(face))
         signed_v[...] = zflat[...].astype(BF16)
         forward, finish = forward_next, finish_next
     for axis in range(3):
@@ -1113,6 +1156,7 @@
                     dma((plane * nz,)),
                     dma((plane * nz,)),
                     pltpu.SemaphoreType.REGULAR((max(nx + ny - 2, nz - 1, 2) - 1,)),
+                    pltpu.VMEM((8, cols), F32),
                 ]
                 if narrow
                 else []

time: 43.3 us -> 40.4 us (0.933)
  Pallas kernels: 42.5 us -> 39.6 us
    pallas_call x1, Pallas kernels: 41.5 us -> 38.6 us  [body(): pl.pallas_call(functools.partial(kernel if narrow else kernel_wide, sizes...]
where the time goes in v5:
time: 40.4 us; the launch traced here: 40.2 us
  Pallas kernels  39.6 us (98%)
  between operations  0.64 us (2%)
    pallas_call x1, Pallas kernels, body(): pl.pallas_call(functools.partial(kernel if narrow else kernel_wide, sizes...  38.6 us
    pallas_call x1, Pallas kernels, body(): pl.pallas_call(store, out_shape=(out, out), in_specs=[vmem, vmem], out_sp...  0.97 us

profile of v5, /device:TPU:0, one launch (start us, length us, event | category | flops | bytes accessed | tf_op | source)
XLA Modules:
  0.0 40.2 jit_solution(15945024211620348298)
XLA Ops:
  0.6 38.6 %shard_map.77 = (f32[3,300,128]{2,1,0:T(8,128)S(1)}, f32[3,300,128]{2,1,0:T(8,128)S(1)}) custom-call(f32[3,300,1,128]{3,2,1,0:T(1,128)} %bitcast.13, bf16[1800,1800]{1,0:T(8,128)(2,1)} %bitcast.11, bf16[24,1800]{1,0:T(8,128)(2,1)} %bitcast.14, bf16[6,300,300]{2,1,0:T(8,128)(2,1)} %bitcast.12, bf16[27,27]{1,0:T(8,128)(2,1)} %cinv_hbm.1, s32[8]{0:T(128)} %bitcast.15), custom_call_target="tpu_custom_call" | custom-call | tf_op jit(solution)/shard_map/pallas_call | solution.py:1086
  39.2 1.0 %shard_map.78 = (f32[3,300,1,128]{3,2,1,0:T(1,128)}, f32[3,300,1,128]{3,2,1,0:T(1,128)}) custom-call(f32[3,300,128]{2,1,0:T(8,128)S(1)} %get-tuple-element.6.mult_ref, f32[3,300,128]{2,1,0:T(8,128)S(1)} %get-tuple-element.7.resid_ref), custom_call_target="tpu_custom_call" | custom-call | tf_op jit(solution)/shard_map/pallas_call | solution.py:1169
